TPU v7x, 32 devices: a whole 2x2x4 slice. The times are simulated.
32 devices in a mesh: head: 4 (over z), seq: 8 (over y, x, core).
Axes of the slice: x: 2, y: 2, z: 4, core: 2. Of those that a mesh axis runs over, the one named last changes fastest.
Arguments:
- queries: bfloat16 [1024, 8192], P('seq', 'head'), may hold values from -100 to 100
- keys: bfloat16 [1024, 1024], P('seq', 'head'), may hold values from -5 to 5
- values: bfloat16 [1024, 1024], P('seq', 'head'), may hold values from -6 to 6
- q_tangent: bfloat16 [1024, 8192], P('seq', 'head'), may hold values from -6 to 6
- k_tangent: bfloat16 [1024, 1024], P('seq', 'head'), may hold values from -6 to 6
- v_tangent: bfloat16 [1024, 1024], P('seq', 'head'), may hold values from -6 to 6
- out_grad: bfloat16 [1024, 8192], P('seq', 'head'), may hold values from -6 to 6
- block_order: int32 [8], replicated, may hold values from 0 to 7, each once
Outputs:
- dq_tangent: bfloat16 [1024, 8192], P('seq', 'head')
- dk_tangent: bfloat16 [1024, 1024], P('seq', 'head')
- dv_tangent: bfloat16 [1024, 1024], P('seq', 'head')
- squared_norm: float32 [], replicated
Inputs may be any that keep to these rules, and one draw needn't show every extreme that they name: `block_order`: every value of 0 to 7 appears once.
All inputs are finite; a program needn't handle non-finite values.
Results may differ from a plain program's by a relative error of at most 0.025.
Values may be sent and summed in bfloat16 or wider, within the bound.
No kernel may reach another device: no remote copies, remote signals or barrier semaphores. Data moves between devices by JAX's collectives and lax.ppermute only.
A program may use at most 64 MiB of HBM per device.

v0:
```python
import functools

import jax
import jax.numpy as jnp
from jax import lax
from jax.experimental import pallas as pl
from jax.experimental.pallas import tpu as pltpu
from jax.sharding import PartitionSpec as P

HD = 128
G = 8
ROWS = 256
CHUNK = 256
LOG2E = 1.4426950408889634
FILL = -1e30

NT = (((1,), (1,)), ((), ()))
NN = (((1,), (0,)), ((), ()))


def dot(a, b, dims):
    return lax.dot_general(a, b, dims, preferred_element_type=jnp.float32)


def hvp_kernel(
    seq_of, out_seq, n_kv, n_out, tokens, width, col_of, scaling,
    me_ref, order_ref, q_ref, qt_ref, do_ref, peer_ref, *rest
):
    kv_refs = rest[:n_kv]
    dq_ref, sq_ref = rest[n_kv : n_kv + 2]
    out_refs = rest[n_kv + 2 : n_kv + 2 + n_out]
    rest = rest[n_kv + 2 + n_out :]
    (qs, kvs, kts, x_s, dq_acc, acc, sem, mc_a, mc_b) = rest[:9]
    slot_a, slot_b = rest[9:13], rest[13:]
    groups = width // HD
    tiles = width // ROWS
    per_tile = ROWS // tokens
    me = me_ref[0]
    first = col_of(me)

    copies = []
    for which, ref in enumerate((q_ref, qt_ref, do_ref)):
        for g in range(groups):
            copies.append(
                pltpu.make_async_copy(
                    ref.at[:, pl.ds(pl.multiple_of(first + g * HD, HD), HD)],
                    qs.at[0, g // per_tile, which, pl.ds((g % per_tile) * tokens, tokens), :],
                    sem.at[0],
                )
            )
            copies.append(
                pltpu.make_async_copy(
                    peer_ref.at[:, pl.ds(which * width + g * HD, HD)],
                    qs.at[1, g // per_tile, which, pl.ds((g % per_tile) * tokens, tokens), :],
                    sem.at[0],
                )
            )
    for m, ref in enumerate(kv_refs):
        for e in range(ref.shape[0]):
            copies.append(
                pltpu.make_async_copy(
                    ref.at[e], kvs.at[order_ref[seq_of(me, m, e)]], sem.at[0]
                )
            )
    for c in copies:
        c.start()
    acc[...] = jnp.zeros_like(acc)
    sq_ref[...] = jnp.zeros_like(sq_ref)
    for c in copies:
        c.wait()

    blocks = kvs.shape[0]
    per_chunk = CHUNK // tokens
    chunks = blocks // per_chunk

    def chunk_kv(kc):
        return kvs[pl.ds(kc * per_chunk, per_chunk)].reshape(CHUNK, 4 * HD)

    def transpose_keys(kc, _):
        kv = chunk_kv(kc)
        kts[kc] = jnp.concatenate([kv[:, :HD].T, kv[:, HD : 2 * HD].T], axis=1)
        return 0

    lax.fori_loop(0, chunks, transpose_keys, 0)

    scale2 = scaling * LOG2E
    key_iota = lax.broadcasted_iota(jnp.int32, (CHUNK, ROWS), 0)
    row_iota = lax.rem(lax.broadcasted_iota(jnp.int32, (CHUNK, ROWS), 1), tokens)
    behind = row_iota - key_iota

    def split(x):
        return x.reshape(x.shape[0] // 8, 8, x.shape[1])

    piece = 32

    def score_dots(t_rows, slot, kc, masked, b):
        q, qt, do = t_rows
        s_s, st_s, dp_s, dpt_s = slot
        kv = chunk_kv(kc)
        s = dot(kv[:, :HD], q, NT)
        if masked:
            s = jnp.where(behind >= kc * CHUNK - b * tokens, s, FILL)
        s_s[kc] = s
        st_s[kc] = dot(kv[:, : 2 * HD], jnp.concatenate([qt, q], axis=1), NT)
        dp_s[kc] = dot(kv[:, 2 * HD : 3 * HD], do, NT)
        dpt_s[kc] = dot(kv[:, 3 * HD :], do, NT)

    def score_sums(slot, mc_s, kc, stats):
        s_s, st_s, dp_s, dpt_s = slot
        m_old, z, s1, d1, x1, y1 = stats
        m_new = m_old
        for k in range(0, CHUNK, piece):
            s = split(s_s[kc, k : k + piece])
            m_new = jnp.maximum(m_new, jnp.max(s, axis=0) * scale2)
        decay = jnp.exp2(m_old - m_new)
        mc_s[kc] = m_new
        z, s1, d1, x1, y1 = [v * decay for v in (z, s1, d1, x1, y1)]
        for k in range(0, CHUNK, piece):
            at = slice(k, k + piece)
            e = jnp.exp2(split(s_s[kc, at]) * scale2 - m_new[None])
            s_s[kc, at] = e.reshape(piece, ROWS)
            est = e * split(st_s[kc, at])
            dp = split(dp_s[kc, at])
            z = z + jnp.sum(e, axis=0)
            s1 = s1 + jnp.sum(est, axis=0)
            d1 = d1 + jnp.sum(e * dp, axis=0)
            x1 = x1 + jnp.sum(est * dp, axis=0)
            y1 = y1 + jnp.sum(e * split(dpt_s[kc, at]), axis=0)
        return (m_new, z, s1, d1, x1, y1)

    def finish(stats):
        m8, z, s1, d1, x1, y1 = stats
        top = jnp.max(m8, axis=0, keepdims=True)
        w8 = jnp.exp2(m8 - top)

        def total(v):
            return jnp.sum(v * w8, axis=0, keepdims=True)

        rz = 1.0 / total(z)
        tan_mean = total(s1) * rz
        delta = total(d1) * rz
        delta_tan = scaling * (total(x1) * rz - tan_mean * delta) + total(y1) * rz
        return (top, rz, tan_mean, delta, delta_tan)

    def grad_values(slot, mc_s, kc, done):
        s_s, st_s, dp_s, dpt_s = slot
        top, rz, tan_mean, delta, delta_tan = done
        f = jnp.exp2(mc_s[kc] - top) * rz
        fc = f * scaling
        for k in range(0, CHUNK, piece):
            at = slice(k, k + piece)
            e = split(s_s[kc, at])
            p = e * f[None]
            pt = e * fc[None] * (split(st_s[kc, at]) - tan_mean[None])
            dd = split(dp_s[kc, at]) - delta[None]
            dst = pt * dd + p * (split(dpt_s[kc, at]) - delta_tan[None])
            for j, v in enumerate((dst, p * dd, pt)):
                x_s[j, at] = v.reshape(piece, ROWS).astype(jnp.bfloat16)

    def grad_dots(t_rows, kc):
        q, qt, do = t_rows
        dst, ds, pt = x_s[0], x_s[1], x_s[2]
        dq_acc[...] += dot(kts[kc], jnp.concatenate([dst, ds], axis=0), NN)
        dk = dot(jnp.concatenate([dst, ds], axis=1), jnp.concatenate([q, qt], axis=0), NN)
        dv = dot(pt, do, NN)
        at = pl.ds(kc * per_chunk, per_chunk)
        acc[at] += jnp.concatenate([dk, dv], axis=1).reshape(per_chunk, tokens, 2 * HD)

    slots = (slot_a, slot_b)
    mcs = (mc_a, mc_b)
    zero = jnp.zeros((8, ROWS), jnp.float32)
    start = (jnp.full((8, ROWS), FILL, jnp.float32), zero, zero, zero, zero, zero)

    def block(i, _):
        b = order_ref[jnp.where(i == 0, me, me ^ 1)]
        full = (b * tokens) // CHUNK

        def rows(t):
            return (qs[i, t, 0], qs[i, t, 1], qs[i, t, 2])

        def step(kc, stats, t, done, masked):
            now, nxt = t % 2, (t + 1) % 2
            if done is not None:
                grad_values(slots[now], mcs[now], kc, done)
            if t + 1 < tiles:
                score_dots(rows(t + 1), slots[nxt], kc, masked, b)
            if done is not None:
                grad_dots(rows(t), kc)
            if t + 1 < tiles:
                stats = score_sums(slots[nxt], mcs[nxt], kc, stats)
            return stats

        done = None
        for t in range(-1, tiles):
            if done is not None:
                dq_acc[...] = jnp.zeros_like(dq_acc)
            if t + 1 < tiles:
                stats = lax.fori_loop(
                    0, full, functools.partial(step, t=t, done=done, masked=False), start
                )
                stats = step(full, stats, t, done, True)
            else:
                stats = lax.fori_loop(
                    0, full + 1, functools.partial(step, t=t, done=done, masked=False), start
                )
            if done is not None:
                dq = (dq_acc[...] * scaling).T.astype(jnp.bfloat16)
                wide = dq.astype(jnp.float32)
                sq_ref[...] += jnp.sum(split(wide * wide), axis=0)
                for h in range(per_tile):
                    part = dq[h * tokens : (h + 1) * tokens]
                    c = (t * per_tile + h) * HD
                    dq_ref[i, :, c : c + HD] = part
            done = finish(stats)
        return 0

    lax.fori_loop(0, 2, block, 0)

    for m, ref in enumerate(out_refs):
        for e in range(ref.shape[0] // tokens):
            block_at = acc[order_ref[out_seq(me, m, e)]]
            rows_at = slice(e * tokens, (e + 1) * tokens)
            ref[rows_at, :HD] = (block_at[:, :HD] * scaling).astype(ref.dtype)
            ref[rows_at, HD:] = block_at[:, HD:].astype(ref.dtype)


def run_hvp(me, order, q, qt, do, peer, kvs, outs, seq_of, out_seq, col_of, width):
    tokens = q.shape[0]
    blocks = sum(k.shape[0] for k in kvs)
    chunks = blocks * tokens // CHUNK
    tiles = width // ROWS
    f32 = jnp.float32
    score = pltpu.VMEM((chunks, CHUNK, ROWS), f32)
    kernel = functools.partial(
        hvp_kernel, seq_of, out_seq, len(kvs), len(outs), tokens, width, col_of, HD ** (-0.5)
    )
    outs = [
        jax.ShapeDtypeStruct((2, tokens, width), jnp.bfloat16),
        jax.ShapeDtypeStruct((8, HD), f32),
    ] + outs
    flops = 2 * blocks * tokens * tokens * width * 10
    return pl.pallas_call(
        kernel,
        name="hvp",
        out_shape=outs,
        in_specs=[pl.BlockSpec(memory_space=pltpu.SMEM)] * 2
        + [pl.BlockSpec(memory_space=pl.ANY)] * (4 + len(kvs)),
        out_specs=[pl.BlockSpec(memory_space=pltpu.VMEM)] * len(outs),
        scratch_shapes=[
            pltpu.VMEM((2, tiles, 3, ROWS, HD), jnp.bfloat16),
            pltpu.VMEM((blocks, tokens, 4 * HD), jnp.bfloat16),
            pltpu.VMEM((chunks, HD, 2 * CHUNK), jnp.bfloat16),
            pltpu.VMEM((3, CHUNK, ROWS), jnp.bfloat16),
            pltpu.VMEM((HD, ROWS), f32),
            pltpu.VMEM((blocks, tokens, 2 * HD), f32),
            pltpu.SemaphoreType.DMA((1,)),
            pltpu.VMEM((chunks, 8, ROWS), f32),
            pltpu.VMEM((chunks, 8, ROWS), f32),
        ]
        + [score] * 8,
        compiler_params=pltpu.CompilerParams(vmem_limit_bytes=48 * 1024 * 1024),
        cost_estimate=pl.CostEstimate(flops=flops, bytes_accessed=4 << 20, transcendentals=0),
    )(me, order, q, qt, do, peer, *kvs)


def join_kernel(copies, me_ref, own_ref, *rest):
    got = rest[: copies - 1]
    dq_ref, dq_got_ref, sq_ref, dq_out, dk_out, dv_out, sum_ref, sem = rest[copies - 1 :]
    width = dq_ref.shape[2]
    core = lax.rem(me_ref[0], 2)
    mine = pl.multiple_of(core * width, HD)
    theirs = pl.multiple_of((1 - core) * width, HD)
    moves = (
        pltpu.make_async_copy(dq_ref.at[0], dq_out.at[:, pl.ds(mine, width)], sem.at[0]),
        pltpu.make_async_copy(dq_got_ref, dq_out.at[:, pl.ds(theirs, width)], sem.at[1]),
    )
    for move in moves:
        move.start()
    f32 = jnp.float32
    total = sq_ref[...]
    for side in range(2):
        at = pl.ds(pl.multiple_of((core if side == 0 else 1 - core) * HD, HD), HD)
        for half, out in enumerate((dk_out, dv_out)):
            cols = slice(half * HD, (half + 1) * HD)
            parts = [got[m - 1][:, cols].astype(f32) for m in range(2 - side, copies, 2)]
            if side == 0:
                parts = [own_ref[:, cols]] + parts
            final = sum(parts[1:], parts[0]).astype(jnp.bfloat16)
            out[:, at] = final
            wide = final.astype(f32)
            total = total + jnp.sum((wide * wide).reshape(-1, 8, HD), axis=0)
    line = jnp.sum(total, axis=0, keepdims=True)
    sum_ref[...] = jnp.broadcast_to(line[None], sum_ref.shape)
    for move in moves:
        move.wait()


def run_join(me, own, got, dq, dq_got, sq, devices):
    tokens, cols = own.shape
    width = dq.shape[2]
    half = jax.ShapeDtypeStruct((tokens, 2 * HD), jnp.bfloat16)
    return pl.pallas_call(
        functools.partial(join_kernel, len(got) + 1),
        name="join",
        out_shape=[
            jax.ShapeDtypeStruct((tokens, 2 * width), jnp.bfloat16),
            half,
            half,
            jax.ShapeDtypeStruct((devices, 1, HD), jnp.float32),
        ],
        in_specs=[pl.BlockSpec(memory_space=pltpu.SMEM)]
        + [pl.BlockSpec(memory_space=pltpu.VMEM)] * (len(got) + 4),
        out_specs=[pl.BlockSpec(memory_space=pl.ANY)]
        + [pl.BlockSpec(memory_space=pltpu.VMEM)] * 3,
        scratch_shapes=[pltpu.SemaphoreType.DMA((2,))],
        cost_estimate=pl.CostEstimate(flops=1 << 20, bytes_accessed=2 << 20, transcendentals=0),
    )(me, own, *got, dq, dq_got, sq)


def shifted(x, axis, bit):
    size = lax.axis_size(axis)
    return lax.ppermute(x, axis, [(i, i ^ bit) for i in range(size)])


def all_sum(x, axes):
    for axis in axes:
        size = lax.axis_size(axis)
        if size & (size - 1):
            x = lax.psum(x, axis)
            continue
        bit = 1
        while bit < size:
            x = x + shifted(x, axis, bit)
            bit *= 2
    return x


def square_sum(x):
    w = x.astype(jnp.float32)
    return jnp.sum(w * w)


def join(core, mine, theirs):
    low = jnp.where(core == 0, mine, theirs)
    high = jnp.where(core == 0, theirs, mine)
    return jnp.concatenate([low, high], axis=1)


def body(queries, keys, values, q_tangent, k_tangent, v_tangent, out_grad, block_order):
    tokens = queries.shape[0]
    heads = keys.shape[1] // HD
    shards = lax.axis_size("seq")
    me = lax.axis_index("seq").astype(jnp.int32)
    core = lax.rem(me, 2)
    me_arr = me.reshape(1)
    width = heads * G * HD // 2
    other = (1 - core) * width
    f32 = jnp.float32

    def swap_rows(arrays):
        cut = [lax.dynamic_slice_in_dim(x, other, width, 1) for x in arrays]
        return shifted(jnp.concatenate(cut, axis=1), "seq", 1)

    rows = (queries, q_tangent, out_grad)

    def col_of(at):
        return lax.rem(at, 2) * width

    def pack(head):
        return jnp.concatenate(
            [
                lax.dynamic_slice_in_dim(x, head * HD, HD, 1)
                for x in (keys, k_tangent, values, v_tangent)
            ],
            axis=1,
        )

    if heads == 2 and shards == 8:
        mine = pack(core)
        theirs = shifted(pack(1 - core), "seq", 1)
        chip = jnp.stack([mine, theirs])
        *late, _ = lax.optimization_barrier((*rows, theirs))
        x_kv = shifted(chip, "seq", 2)
        y_kv = shifted(chip, "seq", 4)
        peer_rows = swap_rows(late)
        half = 2 * HD
        xy_a = shifted(y_kv[:, :, :half], "seq", 2)
        xy_b = shifted(x_kv[:, :, half:], "seq", 4)
        xy_kv = jnp.concatenate([xy_a, xy_b], axis=2)
        dq, sq, own, *parts = run_hvp(
            me_arr, block_order, *rows, peer_rows, (chip, x_kv, y_kv, xy_kv),
            [jax.ShapeDtypeStruct((tokens, 2 * HD), f32)]
            + [jax.ShapeDtypeStruct((tokens, 2 * HD), jnp.bfloat16)] * (shards - 1),
            lambda at, m, e: at ^ (2 * m + e), lambda at, m, e: at ^ m, col_of, width,
        )
        got = [shifted(p, "seq", m + 1) for m, p in enumerate(parts)]
        dq_got = shifted(dq[1], "seq", 1)
        devices = shards * lax.axis_size("head")
        dq_out, dk_out, dv_out, line = run_join(me_arr, own, got, dq, dq_got, sq, devices)
        line = lax.all_to_all(line, ("head", "seq"), 0, 0)
        return (dq_out, dk_out, dv_out, jnp.sum(line))
    assert heads == 1
    whole = lax.all_gather(pack(0), "seq", axis=0)
    dq, sq, parts = run_hvp(
        me_arr, block_order, *rows, swap_rows(rows), (whole,),
        [jax.ShapeDtypeStruct((shards * tokens, 2 * HD), jnp.bfloat16)],
        lambda at, m, e: e, lambda at, m, e: e, col_of, width,
    )
    final = lax.psum_scatter(parts, "seq", scatter_dimension=0, tiled=True)
    dq_out = join(core, dq[0], shifted(dq[1], "seq", 1))
    local = square_sum(final) + jnp.sum(sq)
    squared_norm = all_sum(local, ("seq", "head"))
    return (dq_out, final[:, :HD], final[:, HD:], squared_norm)


def solution(mesh):
    placed = (P("seq", "head"),) * 7 + (P(),)
    return jax.shard_map(
        body,
        mesh=mesh,
        in_specs=placed,
        out_specs=(P("seq", "head"), P("seq", "head"), P("seq", "head"), P()),
        check_vma=False,
    )
```

profile of v0, /device:TPU:0, one launch (start us, length us, event | category | flops | bytes accessed | tf_op | source)
XLA Modules:
  0.0 69.6 jit_solution(14828906716289018799)
XLA Ops:
  0.6 0.0 copy-start.2
  0.6 0.0 copy-start.3
  0.7 0.9 %constant_dynamic-slice_fusion.2 = (bf16[128,128]{1,0:T(8,128)(2,1)S(1)}, bf16[128,128]{1,0:T(8,128)(2,1)S(1)}, bf16[128,128]{1,0:T(8,128)(2,1)S(1)}, bf16[128,128]{1,0:T(8,128)(2,1)S(1)}) fusion(bf16[128,256]{1,0:T(8,128)(2,1)} %param.12, s32[]{:T(128)S(6)} %select_n.8, s32[]{:T(128)S(6)} %select_n.6, bf16[128,256]{1,0:T(8,128)(2,1)} %param.9), kind=kLoop, calls=%fused_computation.8 | loop fusion | bytes 262152 | tf_op jit(solution)/shard_map/dynamic_slice | solution.py:372
  1.6 0.0 copy-start.4
  1.6 0.9 %constant_dynamic-slice_fusion = (bf16[128,128]{1,0:T(8,128)(2,1)S(1)}, bf16[128,128]{1,0:T(8,128)(2,1)S(1)}, bf16[128,128]{1,0:T(8,128)(2,1)S(1)}, bf16[128,128]{1,0:T(8,128)(2,1)S(1)}) fusion(bf16[128,256]{1,0:T(8,128)(2,1)} %param.13, s32[]{:T(128)S(6)} %select_n.8, s32[]{:T(128)S(6)} %select_n.6, bf16[128,256]{1,0:T(8,128)(2,1)} %param.10), kind=kLoop, calls=%fused_computation.6 | loop fusion | bytes 262152 | tf_op jit(solution)/shard_map/dynamic_slice | solution.py:372
  2.5 0.6 collective-permute-start
  3.1 1.0 %collective-permute-done = bf16[128,512]{1,0:T(8,128)(2,1)S(1)} collective-permute-done((bf16[128,512]{1,0:T(8,128)(2,1)S(1)}, bf16[128,512]{1,0:T(8,128)(2,1)S(1)}, u32[]{:S(2)}, u32[]{:S(2)}) %collective-permute-start) | collective-permute-done | bytes 131104 | tf_op jit(solution)/shard_map/ppermute | solution.py:322
  4.0 0.0 copy-done.2
  4.1 0.0 copy-done.3
  4.1 0.0 copy-done.4
  4.2 0.1 pad_maximum_fusion
  4.2 0.4 collective-permute-start.1
  4.7 0.0 copy-start.6
  4.7 2.7 %collective-permute-start.3 = (bf16[2,128,512]{2,1,0:T(8,128)(2,1)S(1)}, bf16[2,128,512]{2,1,0:T(8,128)(2,1)S(1)}, u32[]{:S(2)}, u32[]{:S(2)}) collective-permute-start(bf16[2,128,512]{2,1,0:T(8,128)(2,1)S(1)} %pad_maximum_fusion.1.rest_0_), channel_id=1, source_target_pairs={{0,4},{1,5},{2,6},{3,7},{4,0},{5,1},{6,2},{7,3},{8,12},{9,13},{10,... | collective-permute-start | bytes 786440 | tf_op jit(solution)/shard_map/ppermute | solution.py:322
  7.4 1.5 %collective-permute-start.2 = (bf16[2,128,512]{2,1,0:T(8,128)(2,1)S(1)}, bf16[2,128,512]{2,1,0:T(8,128)(2,1)S(1)}, u32[]{:S(2)}, u32[]{:S(2)}) collective-permute-start(bf16[2,128,512]{2,1,0:T(8,128)(2,1)S(1)} %pad_maximum_fusion.1.rest_0_), channel_id=1, source_target_pairs={{0,2},{1,3},{2,0},{3,1},{4,6},{5,7},{6,4},{7,5},{8,10},{9,11},{10,... | collective-permute-start | bytes 786440 | tf_op jit(solution)/shard_map/ppermute | solution.py:322
  8.9 5.3 %collective-permute-done.3.rest_2_ = bf16[2,128,512]{2,1,0:T(8,128)(2,1)S(1)} collective-permute-done((bf16[2,128,512]{2,1,0:T(8,128)(2,1)S(1)}, bf16[2,128,512]{2,1,0:T(8,128)(2,1)S(1)}, u32[]{:S(2)}, u32[]{:S(2)}) %collective-permute-start.3) | collective-permute-done | bytes 262176 | tf_op jit(solution)/shard_map/ppermute | solution.py:322
  14.3 1.8 %collective-permute-start.4 = (bf16[2,128,256]{2,1,0:T(8,128)(2,1)S(1)}, bf16[2,128,256]{2,1,0:T(8,128)(2,1)S(1)}, u32[]{:S(2)}, u32[]{:S(2)}) collective-permute-start(bf16[2,128,256]{2,1,0:T(8,128)(2,1)S(1)} %slice.12), channel_id=1, source_target_pairs={{0,2},{1,3},{2,0},{3,1},{4,6},{5,7},{6,4},{7,5},{8,10},{9,11},{10,... | collective-permute-start | bytes 393224 | tf_op jit(solution)/shard_map/ppermute | solution.py:322
  16.1 0.0 collective-permute-done.2.rest_1_
  16.1 1.6 %collective-permute-start.5 = (bf16[2,128,256]{2,1,0:T(8,128)(2,1)S(1)}, bf16[2,128,256]{2,1,0:T(8,128)(2,1)S(1)}, u32[]{:S(2)}, u32[]{:S(2)}) collective-permute-start(bf16[2,128,256]{2,1,0:T(8,128)(2,1)S(1)} %slice.13), channel_id=1, source_target_pairs={{0,4},{1,5},{2,6},{3,7},{4,0},{5,1},{6,2},{7,3},{8,12},{9,13},{10,... | collective-permute-start | bytes 393224 | tf_op jit(solution)/shard_map/ppermute | solution.py:322
  17.7 1.9 %collective-permute-done.4 = bf16[2,128,256]{2,1,0:T(8,128)(2,1)S(1)} collective-permute-done((bf16[2,128,256]{2,1,0:T(8,128)(2,1)S(1)}, bf16[2,128,256]{2,1,0:T(8,128)(2,1)S(1)}, u32[]{:S(2)}, u32[]{:S(2)}) %collective-permute-start.4) | collective-permute-done | bytes 131104 | tf_op jit(solution)/shard_map/ppermute | solution.py:322
  19.5 1.6 %collective-permute-done.5 = bf16[2,128,256]{2,1,0:T(8,128)(2,1)S(1)} collective-permute-done((bf16[2,128,256]{2,1,0:T(8,128)(2,1)S(1)}, bf16[2,128,256]{2,1,0:T(8,128)(2,1)S(1)}, u32[]{:S(2)}, u32[]{:S(2)}) %collective-permute-start.5) | collective-permute-done | bytes 131104 | tf_op jit(solution)/shard_map/ppermute | solution.py:322
  21.1 0.0 collective-permute-done.1.peer_ref
  21.1 0.0 copy-done.6
  21.1 12.7 %hvp.1 = (bf16[2,128,1024]{2,1,0:T(8,128)(2,1)S(1)}, f32[8,128]{1,0:T(8,128)S(1)}, f32[128,256]{1,0:T(8,128)S(1)}, bf16[128,256]{1,0:T(8,128)(2,1)S(1)}, bf16[12...) custom-call(s32[1]{0:T(128)} %bitcast.me_ref, ...), custom_call_target="tpu_custom_call" | custom-call | flops 2684354560 | bytes 4194304 | tf_op jit(solution)/shard_map/hvp/pallas_call | solution.py:242
  33.9 0.0 copy-start.1
  33.9 0.6 copy-done.1
  34.5 0.0 copy-start.5
  34.5 0.6 copy-done.5
  35.1 0.0 copy-start
  35.2 0.1 collective-permute-start.13
  35.2 0.5 collective-permute-start.6
  35.7 8.2 %collective-permute-start.7 = (bf16[128,256]{1,0:T(8,128)(2,1)S(1)}, bf16[128,256]{1,0:T(8,128)(2,1)S(1)}, u32[]{:S(2)}, u32[]{:S(2)}) collective-permute-start(bf16[128,256]{1,0:T(8,128)(2,1)S(1)} %get-tuple-element.26), channel_id=1, source_target_pairs={{0,2},{1,3},{2,0},{3,1},{4,6},{5,7},{6,4},{7,5},{8,10},{9,11},{10,... | collective-permute-start | bytes 196616 | tf_op jit(solution)/shard_map/ppermute | solution.py:322
  43.9 0.0 collective-permute-start.8
  43.9 0.0 collective-permute-start.9
  43.9 0.0 collective-permute-done.6.rest_0_
  43.9 0.0 copy-start.8
  43.9 1.5 %collective-permute-start.10 = (bf16[128,256]{1,0:T(8,128)(2,1)S(1)}, bf16[128,256]{1,0:T(8,128)(2,1)S(1)}, u32[]{:S(2)}, u32[]{:S(2)}) collective-permute-start(bf16[128,256]{1,0:T(8,128)(2,1)S(1)} %get-tuple-element.29), channel_id=1, source_target_pairs={{0,5},{1,4},{2,7},{3,6},{4,1},{5,0},{6,3},{7,2},{8,13},{9,12},{10,... | collective-permute-start | bytes 196616 | tf_op jit(solution)/shard_map/ppermute | solution.py:322
  45.4 0.9 %collective-permute-done.7.rest_1_ = bf16[128,256]{1,0:T(8,128)(2,1)S(1)} collective-permute-done((bf16[128,256]{1,0:T(8,128)(2,1)S(1)}, bf16[128,256]{1,0:T(8,128)(2,1)S(1)}, u32[]{:S(2)}, u32[]{:S(2)}) %collective-permute-start.7) | collective-permute-done | bytes 65568 | tf_op jit(solution)/shard_map/ppermute | solution.py:322
  46.3 0.0 copy-start.9
  46.3 1.0 %collective-permute-start.11 = (bf16[128,256]{1,0:T(8,128)(2,1)S(1)}, bf16[128,256]{1,0:T(8,128)(2,1)S(1)}, u32[]{:S(2)}, u32[]{:S(2)}) collective-permute-start(bf16[128,256]{1,0:T(8,128)(2,1)S(1)} %get-tuple-element.30), channel_id=1, source_target_pairs={{0,6},{1,7},{2,4},{3,5},{4,2},{5,3},{6,0},{7,1},{8,14},{9,15},{10,... | collective-permute-start | bytes 196616 | tf_op jit(solution)/shard_map/ppermute | solution.py:322
  47.2 1.1 %collective-permute-done.8.rest_2_ = bf16[128,256]{1,0:T(8,128)(2,1)S(1)} collective-permute-done((bf16[128,256]{1,0:T(8,128)(2,1)S(1)}, bf16[128,256]{1,0:T(8,128)(2,1)S(1)}, u32[]{:S(2)}, u32[]{:S(2)}) %collective-permute-start.8) | collective-permute-done | bytes 65568 | tf_op jit(solution)/shard_map/ppermute | solution.py:322
  48.3 0.0 copy-start.10
  48.3 0.0 collective-permute-start.12
  48.3 0.4 collective-permute-done.9.rest_3_
  48.7 0.0 copy-start.11
  48.7 0.0 collective-permute-done.10.rest_4_
  48.7 0.0 copy-start.12
  48.8 2.7 %collective-permute-done.11.rest_5_ = bf16[128,256]{1,0:T(8,128)(2,1)S(1)} collective-permute-done((bf16[128,256]{1,0:T(8,128)(2,1)S(1)}, bf16[128,256]{1,0:T(8,128)(2,1)S(1)}, u32[]{:S(2)}, u32[]{:S(2)}) %collective-permute-start.11) | collective-permute-done | bytes 65568 | tf_op jit(solution)/shard_map/ppermute | solution.py:322
  51.4 0.0 copy-start.13
  51.4 1.9 %collective-permute-done.12.rest_6_ = bf16[128,256]{1,0:T(8,128)(2,1)S(1)} collective-permute-done((bf16[128,256]{1,0:T(8,128)(2,1)S(1)}, bf16[128,256]{1,0:T(8,128)(2,1)S(1)}, u32[]{:S(2)}, u32[]{:S(2)}) %collective-permute-start.12) | collective-permute-done | bytes 65568 | tf_op jit(solution)/shard_map/ppermute | solution.py:322
  53.3 0.0 collective-permute-done.13.rest_8_
  53.3 0.0 copy-start.7
  53.3 0.0 copy-done
  53.3 0.0 copy-done.8
  53.3 0.0 copy-done.9
  53.4 0.0 copy-done.10
  53.4 0.0 copy-done.11
  53.4 0.0 copy-done.12
  53.4 0.0 copy-done.13
  53.4 0.6 copy-done.14
  54.0 0.1 copy-done.7
  54.1 2.8 %join.1 = (bf16[128,2048]{1,0:T(8,128)(2,1)}, bf16[128,256]{1,0:T(8,128)(2,1)}, bf16[128,256]{1,0:T(8,128)(2,1)}, f32[32,1,128]{2,1,0:T(1,128)}) custom-call(s32[1]{0:T(128)} %bitcast.me_ref, f32[128,256]{1,0:T(8,128)} %copy-done.1, bf16[128,256]{1,0:T(8,128)(2,1)} %copy-done.8, bf16[128,256]{1,0:T(8,128)(2,1)} %copy-done.9, bf16[128,256]{1,0:T(8,128)(2,1)} %copy-done.10, ...), custom_call_target="tpu_custom_call" | custom-call | flops 1048576 | bytes 2097152 | tf_op jit(solution)/shard_map/join/pallas_call | solution.py:302
  56.9 12.0 %all_to_all.5 = f32[32,1,128]{2,1,0:T(1,128)S(1)} all-to-all(f32[32,1,128]{2,1,0:T(1,128)} %get-tuple-element.37), channel_id=1, replica_groups=mesh['head'=4,'seq'=8] {'head','seq'}, dimensions={0} | all-to-all | bytes 32768 | tf_op jit(solution)/shard_map/all_to_all | solution.py:400
  69.0 0.6 reduce_sum.9
  (11 shorter events, 0.2 us)
Async XLA Ops:
  0.6 3.4 %copy-start.2 = (bf16[128,2048]{1,0:T(8,128)(2,1)S(1)}, bf16[128,2048]{1,0:T(8,128)(2,1)}, u32[]{:S(2)}) copy-start(bf16[128,2048]{1,0:T(8,128)(2,1)} %q_ref.1) | copy-start | bytes 1572868
  0.6 3.4 %copy-start.3 = (bf16[128,2048]{1,0:T(8,128)(2,1)S(1)}, bf16[128,2048]{1,0:T(8,128)(2,1)}, u32[]{:S(2)}) copy-start(bf16[128,2048]{1,0:T(8,128)(2,1)} %qt_ref.1) | copy-start | bytes 1572868
  1.6 2.5 %copy-start.4 = (bf16[128,2048]{1,0:T(8,128)(2,1)S(1)}, bf16[128,2048]{1,0:T(8,128)(2,1)}, u32[]{:S(2)}) copy-start(bf16[128,2048]{1,0:T(8,128)(2,1)} %do_ref.1) | copy-start | bytes 1572868
  2.5 1.5 %collective-permute-start = (bf16[128,512]{1,0:T(8,128)(2,1)S(1)}, bf16[128,512]{1,0:T(8,128)(2,1)S(1)}, u32[]{:S(2)}, u32[]{:S(2)}) collective-permute-start(bf16[128,512]{1,0:T(8,128)(2,1)S(1)} %pad_maximum_fusion.3), channel_id=1, source_target_pairs={{0,1},{1,0},{2,3},{3,2},{4,5},{5,4},{6,7},{7,6},{8,9},{9,8},{10,11... | collective-permute-start | bytes 393224 | tf_op jit(solution)/shard_map/ppermute | solution.py:322
  4.2 16.9 %collective-permute-start.1 = (bf16[128,3072]{1,0:T(8,128)(2,1)S(1)}, bf16[128,3072]{1,0:T(8,128)(2,1)S(1)}, u32[]{:S(2)}, u32[]{:S(2)}) collective-permute-start(bf16[128,3072]{1,0:T(8,128)(2,1)S(1)} %pad_maximum_fusion), channel_id=1, source_target_pairs={{0,1},{1,0},{2,3},{3,2},{4,5},{5,4},{6,7},{7,6},{8,9},{9,8},{10,11... | collective-permute-start | bytes 2359304 | tf_op jit(solution)/shard_map/ppermute | solution.py:322
  4.7 16.5 %copy-start.6 = (s32[8]{0:T(128)S(1)}, s32[8]{0:T(128)}, u32[]{:S(2)}) copy-start(s32[8]{0:T(128)} %order_ref.1) | copy-start | bytes 100
  4.7 9.5 %collective-permute-start.3 = (bf16[2,128,512]{2,1,0:T(8,128)(2,1)S(1)}, bf16[2,128,512]{2,1,0:T(8,128)(2,1)S(1)}, u32[]{:S(2)}, u32[]{:S(2)}) collective-permute-start(bf16[2,128,512]{2,1,0:T(8,128)(2,1)S(1)} %pad_maximum_fusion.1.rest_0_), channel_id=1, source_target_pairs={{0,4},{1,5},{2,6},{3,7},{4,0},{5,1},{6,2},{7,3},{8,12},{9,13},{10,... | collective-permute-start | bytes 786440 | tf_op jit(solution)/shard_map/ppermute | solution.py:322
  7.4 8.6 %collective-permute-start.2 = (bf16[2,128,512]{2,1,0:T(8,128)(2,1)S(1)}, bf16[2,128,512]{2,1,0:T(8,128)(2,1)S(1)}, u32[]{:S(2)}, u32[]{:S(2)}) collective-permute-start(bf16[2,128,512]{2,1,0:T(8,128)(2,1)S(1)} %pad_maximum_fusion.1.rest_0_), channel_id=1, source_target_pairs={{0,2},{1,3},{2,0},{3,1},{4,6},{5,7},{6,4},{7,5},{8,10},{9,11},{10,... | collective-permute-start | bytes 786440 | tf_op jit(solution)/shard_map/ppermute | solution.py:322
  14.3 5.3 %collective-permute-start.4 = (bf16[2,128,256]{2,1,0:T(8,128)(2,1)S(1)}, bf16[2,128,256]{2,1,0:T(8,128)(2,1)S(1)}, u32[]{:S(2)}, u32[]{:S(2)}) collective-permute-start(bf16[2,128,256]{2,1,0:T(8,128)(2,1)S(1)} %slice.12), channel_id=1, source_target_pairs={{0,2},{1,3},{2,0},{3,1},{4,6},{5,7},{6,4},{7,5},{8,10},{9,11},{10,... | collective-permute-start | bytes 393224 | tf_op jit(solution)/shard_map/ppermute | solution.py:322
  16.1 5.0 %collective-permute-start.5 = (bf16[2,128,256]{2,1,0:T(8,128)(2,1)S(1)}, bf16[2,128,256]{2,1,0:T(8,128)(2,1)S(1)}, u32[]{:S(2)}, u32[]{:S(2)}) collective-permute-start(bf16[2,128,256]{2,1,0:T(8,128)(2,1)S(1)} %slice.13), channel_id=1, source_target_pairs={{0,4},{1,5},{2,6},{3,7},{4,0},{5,1},{6,2},{7,3},{8,12},{9,13},{10,... | collective-permute-start | bytes 393224 | tf_op jit(solution)/shard_map/ppermute | solution.py:322
  33.9 0.7 copy-start.1
  34.5 0.6 copy-start.5
  35.1 18.2 %copy-start = (bf16[2,128,1024]{2,1,0:T(8,128)(2,1)}, bf16[2,128,1024]{2,1,0:T(8,128)(2,1)S(1)}, u32[]{:S(2)}) copy-start(bf16[2,128,1024]{2,1,0:T(8,128)(2,1)S(1)} %get-tuple-element.32.rest_7_) | copy-start | bytes 1572868
  35.2 18.2 %collective-permute-start.13 = (bf16[128,1024]{1,0:T(8,128)(2,1)S(1)}, bf16[128,1024]{1,0:T(8,128)(2,1)S(1)}, u32[]{:S(2)}, u32[]{:S(2)}) collective-permute-start(bf16[128,1024]{1,0:T(8,128)(2,1)S(1)} %slice_bitcast_fusion), channel_id=1, source_target_pairs={{0,1},{1,0},{2,3},{3,2},{4,5},{5,4},{6,7},{7,6},{8,9},{9,8},{10,11... | collective-permute-start | bytes 786440 | tf_op jit(solution)/shard_map/ppermute | solution.py:322
  35.2 8.7 %collective-permute-start.6 = (bf16[128,256]{1,0:T(8,128)(2,1)S(1)}, bf16[128,256]{1,0:T(8,128)(2,1)S(1)}, u32[]{:S(2)}, u32[]{:S(2)}) collective-permute-start(bf16[128,256]{1,0:T(8,128)(2,1)S(1)} %get-tuple-element.25), channel_id=1, source_target_pairs={{0,1},{1,0},{2,3},{3,2},{4,5},{5,4},{6,7},{7,6},{8,9},{9,8},{10,11... | collective-permute-start | bytes 196616 | tf_op jit(solution)/shard_map/ppermute | solution.py:322
  35.7 10.5 %collective-permute-start.7 = (bf16[128,256]{1,0:T(8,128)(2,1)S(1)}, bf16[128,256]{1,0:T(8,128)(2,1)S(1)}, u32[]{:S(2)}, u32[]{:S(2)}) collective-permute-start(bf16[128,256]{1,0:T(8,128)(2,1)S(1)} %get-tuple-element.26), channel_id=1, source_target_pairs={{0,2},{1,3},{2,0},{3,1},{4,6},{5,7},{6,4},{7,5},{8,10},{9,11},{10,... | collective-permute-start | bytes 196616 | tf_op jit(solution)/shard_map/ppermute | solution.py:322
  43.9 4.4 %collective-permute-start.8 = (bf16[128,256]{1,0:T(8,128)(2,1)S(1)}, bf16[128,256]{1,0:T(8,128)(2,1)S(1)}, u32[]{:S(2)}, u32[]{:S(2)}) collective-permute-start(bf16[128,256]{1,0:T(8,128)(2,1)S(1)} %get-tuple-element.27), channel_id=1, source_target_pairs={{0,3},{1,2},{2,1},{3,0},{4,7},{5,6},{6,5},{7,4},{8,11},{9,10},{10,... | collective-permute-start | bytes 196616 | tf_op jit(solution)/shard_map/ppermute | solution.py:322
  43.9 4.8 %collective-permute-start.9 = (bf16[128,256]{1,0:T(8,128)(2,1)S(1)}, bf16[128,256]{1,0:T(8,128)(2,1)S(1)}, u32[]{:S(2)}, u32[]{:S(2)}) collective-permute-start(bf16[128,256]{1,0:T(8,128)(2,1)S(1)} %get-tuple-element.28), channel_id=1, source_target_pairs={{0,4},{1,5},{2,6},{3,7},{4,0},{5,1},{6,2},{7,3},{8,12},{9,13},{10,... | collective-permute-start | bytes 196616 | tf_op jit(solution)/shard_map/ppermute | solution.py:322
  43.9 9.4 %copy-start.8 = (bf16[128,256]{1,0:T(8,128)(2,1)}, bf16[128,256]{1,0:T(8,128)(2,1)S(1)}, u32[]{:S(2)}) copy-start(bf16[128,256]{1,0:T(8,128)(2,1)S(1)} %collective-permute-done.6.rest_0_) | copy-start | bytes 196612
  43.9 4.8 %collective-permute-start.10 = (bf16[128,256]{1,0:T(8,128)(2,1)S(1)}, bf16[128,256]{1,0:T(8,128)(2,1)S(1)}, u32[]{:S(2)}, u32[]{:S(2)}) collective-permute-start(bf16[128,256]{1,0:T(8,128)(2,1)S(1)} %get-tuple-element.29), channel_id=1, source_target_pairs={{0,5},{1,4},{2,7},{3,6},{4,1},{5,0},{6,3},{7,2},{8,13},{9,12},{10,... | collective-permute-start | bytes 196616 | tf_op jit(solution)/shard_map/ppermute | solution.py:322
  46.3 7.1 %copy-start.9 = (bf16[128,256]{1,0:T(8,128)(2,1)}, bf16[128,256]{1,0:T(8,128)(2,1)S(1)}, u32[]{:S(2)}) copy-start(bf16[128,256]{1,0:T(8,128)(2,1)S(1)} %collective-permute-done.7.rest_1_) | copy-start | bytes 196612
  46.3 5.2 %collective-permute-start.11 = (bf16[128,256]{1,0:T(8,128)(2,1)S(1)}, bf16[128,256]{1,0:T(8,128)(2,1)S(1)}, u32[]{:S(2)}, u32[]{:S(2)}) collective-permute-start(bf16[128,256]{1,0:T(8,128)(2,1)S(1)} %get-tuple-element.30), channel_id=1, source_target_pairs={{0,6},{1,7},{2,4},{3,5},{4,2},{5,3},{6,0},{7,1},{8,14},{9,15},{10,... | collective-permute-start | bytes 196616 | tf_op jit(solution)/shard_map/ppermute | solution.py:322
  48.3 5.1 %copy-start.10 = (bf16[128,256]{1,0:T(8,128)(2,1)}, bf16[128,256]{1,0:T(8,128)(2,1)S(1)}, u32[]{:S(2)}) copy-start(bf16[128,256]{1,0:T(8,128)(2,1)S(1)} %collective-permute-done.8.rest_2_) | copy-start | bytes 196612
  48.3 5.0 %collective-permute-start.12 = (bf16[128,256]{1,0:T(8,128)(2,1)S(1)}, bf16[128,256]{1,0:T(8,128)(2,1)S(1)}, u32[]{:S(2)}, u32[]{:S(2)}) collective-permute-start(bf16[128,256]{1,0:T(8,128)(2,1)S(1)} %get-tuple-element.31), channel_id=1, source_target_pairs={{0,7},{1,6},{2,5},{3,4},{4,3},{5,2},{6,1},{7,0},{8,15},{9,14},{10,... | collective-permute-start | bytes 196616 | tf_op jit(solution)/shard_map/ppermute | solution.py:322
  48.7 4.6 %copy-start.11 = (bf16[128,256]{1,0:T(8,128)(2,1)}, bf16[128,256]{1,0:T(8,128)(2,1)S(1)}, u32[]{:S(2)}) copy-start(bf16[128,256]{1,0:T(8,128)(2,1)S(1)} %collective-permute-done.9.rest_3_) | copy-start | bytes 196612
  48.7 4.6 %copy-start.12 = (bf16[128,256]{1,0:T(8,128)(2,1)}, bf16[128,256]{1,0:T(8,128)(2,1)S(1)}, u32[]{:S(2)}) copy-start(bf16[128,256]{1,0:T(8,128)(2,1)S(1)} %collective-permute-done.10.rest_4_) | copy-start | bytes 196612
  51.4 2.0 %copy-start.13 = (bf16[128,256]{1,0:T(8,128)(2,1)}, bf16[128,256]{1,0:T(8,128)(2,1)S(1)}, u32[]{:S(2)}) copy-start(bf16[128,256]{1,0:T(8,128)(2,1)S(1)} %collective-permute-done.11.rest_5_) | copy-start | bytes 196612
  53.3 0.6 copy-start.14
  53.3 0.8 %copy-start.7 = (bf16[128,1024]{1,0:T(8,128)(2,1)}, bf16[128,1024]{1,0:T(8,128)(2,1)S(1)}, u32[]{:S(2)}) copy-start(bf16[128,1024]{1,0:T(8,128)(2,1)S(1)} %collective-permute-done.13.rest_8_) | copy-start | bytes 786436
where the time goes:
time: 70 us; the launch traced here: 69.6 us
  starting transfers between devices  19.8 us (28%)
  waiting for transfers between devices  16.7 us (24%)
  Pallas kernels  15.6 us (22%)
  blocking collectives  12 us (17%)
  local copies, waits for them, and re-layouts  3.87 us (6%)
  between operations  0.89 us (1%)
  other arithmetic  0.77 us (1%)
    ppermute x14, starting transfers between devices, shifted(): return lax.ppermute(x, axis, [(i, i ^ bit) for i in range(size)])  19.8 us
    ppermute x14, waiting for transfers between devices, shifted(): return lax.ppermute(x, axis, [(i, i ^ bit) for i in range(size)])  16.7 us
    pallas_call x1, Pallas kernels, run_hvp(): pl.pallas_call(kernel, name='hvp', out_shape=outs, in_specs=[pl.BlockSpec...  12.7 us
    all_to_all x1, blocking collectives, body(): line = lax.all_to_all(line, ('head', 'seq'), 0, 0)  12 us
    pallas_call x1, Pallas kernels, run_join(): pl.pallas_call(functools.partial(join_kernel, len(got) + 1), name='join',...  2.83 us
    unnamed x30, local copies, waits for them, and re-layouts  1.97 us
    dynamic_slice x2, local copies, waits for them, and re-layouts, pack(): lax.dynamic_slice_in_dim(x, head * HD, HD, 1)  1.79 us
  transfers between devices with their start and end apart: 14, of which 9 were waited for; matrix products, arithmetic and copies ran while one was open for 0% of the time, Pallas kernels for 0%

commit v1 on v0

v1 whole, which is shorter than its diff:
```python
import functools

import jax
import jax.numpy as jnp
from jax import lax
from jax.experimental import pallas as pl
from jax.experimental.pallas import tpu as pltpu
from jax.sharding import PartitionSpec as P

HD = 128
G = 8
ROWS = 256
CHUNK = 256
LOG2E = 1.4426950408889634
FILL = -1e30

NT = (((1,), (1,)), ((), ()))
NN = (((1,), (0,)), ((), ()))


def dot(a, b, dims):
    return lax.dot_general(a, b, dims, preferred_element_type=jnp.float32)


def hvp_kernel(
    seq_of, out_seq, n_own, n_kv, n_out, tokens, width, col_of, scaling,
    me_ref, order_hbm, q_ref, qt_ref, do_ref, peer_ref, *rest
):
    own_kv, rest = rest[:n_own], rest[n_own:]
    kv_refs = rest[:n_kv]
    dq_ref, sq_ref = rest[n_kv : n_kv + 2]
    out_refs = rest[n_kv + 2 : n_kv + 2 + n_out]
    rest = rest[n_kv + 2 + n_out :]
    groups = width // HD
    tiles = width // ROWS
    qs, kvs, kts, acc, sem, stats, order_ref = rest[:7]
    mcs, dqs, xs = (rest[7 + j * tiles : 7 + (j + 1) * tiles] for j in range(3))
    scores = [rest[7 + 3 * tiles + 4 * t :][:4] for t in range(tiles)]
    per_tile = ROWS // tokens
    me = me_ref[0]
    first = col_of(me)

    table = pltpu.make_async_copy(order_hbm, order_ref, sem.at[1])
    table.start()
    copies = []
    for which, ref in enumerate((q_ref, qt_ref, do_ref)):
        for g in range(groups):
            copies.append(
                pltpu.make_async_copy(
                    ref.at[:, pl.ds(pl.multiple_of(first + g * HD, HD), HD)],
                    qs.at[0, g // per_tile, which, pl.ds((g % per_tile) * tokens, tokens), :],
                    sem.at[0],
                )
            )
            copies.append(
                pltpu.make_async_copy(
                    peer_ref.at[:, pl.ds(which * width + g * HD, HD)],
                    qs.at[1, g // per_tile, which, pl.ds((g % per_tile) * tokens, tokens), :],
                    sem.at[0],
                )
            )
    for c in copies:
        c.start()
    table.wait()
    late = []
    for j, ref in enumerate(own_kv):
        head = pl.ds(pl.multiple_of(lax.rem(me, 2) * HD, HD), HD)
        to = kvs.at[order_ref[me], :, pl.ds(j * HD, HD)]
        late.append(pltpu.make_async_copy(ref.at[:, head], to, sem.at[0]))
    for m, ref in enumerate(kv_refs):
        for e in range(ref.shape[0]):
            at = order_ref[seq_of(me, m, e)]
            late.append(pltpu.make_async_copy(ref.at[e], kvs.at[at], sem.at[0]))
    for c in late:
        c.start()
    copies += late
    acc[...] = jnp.zeros_like(acc)
    sq_ref[...] = jnp.zeros_like(sq_ref)
    for c in copies:
        c.wait()

    blocks = kvs.shape[0]
    per_chunk = CHUNK // tokens
    chunks = blocks // per_chunk

    def chunk_kv(kc):
        return kvs[pl.ds(kc * per_chunk, per_chunk)].reshape(CHUNK, 4 * HD)

    def transpose_keys(kc, _):
        kv = chunk_kv(kc)
        kts[kc] = jnp.concatenate([kv[:, :HD].T, kv[:, HD : 2 * HD].T], axis=1)
        return 0

    lax.fori_loop(0, chunks, transpose_keys, 0)

    scale2 = scaling * LOG2E
    key_iota = lax.broadcasted_iota(jnp.int32, (CHUNK, ROWS), 0)
    row_iota = lax.rem(lax.broadcasted_iota(jnp.int32, (CHUNK, ROWS), 1), tokens)
    behind = row_iota - key_iota

    def split(x):
        return x.reshape(x.shape[0] // 8, 8, x.shape[1])

    piece = 32
    span = min(1, tiles)

    def score_dots(i, t, kc, masked, b):
        s_s, st_s, dp_s, dpt_s = scores[t]
        q, qt, do = qs[i, t, 0], qs[i, t, 1], qs[i, t, 2]
        kv = chunk_kv(kc)
        s = dot(kv[:, :HD], q, NT)
        if masked:
            s = jnp.where(behind >= kc * CHUNK - b * tokens, s, FILL)
        s_s[kc] = s
        st_s[kc] = dot(kv[:, : 2 * HD], jnp.concatenate([qt, q], axis=1), NT)
        both = dot(
            jnp.concatenate([kv[:, 2 * HD : 3 * HD], kv[:, 3 * HD :]], axis=0), do, NT
        )
        dp_s[kc] = both[:CHUNK]
        dpt_s[kc] = both[CHUNK:]

    def score_sums(t, kc):
        s_s, st_s, dp_s, dpt_s = scores[t]
        m_old, z, s1, d1, x1, y1 = [stats[t, j] for j in range(6)]
        m_new = m_old
        for k in range(0, CHUNK, piece):
            s = split(s_s[kc, k : k + piece])
            m_new = jnp.maximum(m_new, jnp.max(s, axis=0) * scale2)
        decay = jnp.exp2(m_old - m_new)
        mcs[t][kc] = m_new
        z, s1, d1, x1, y1 = [v * decay for v in (z, s1, d1, x1, y1)]
        for k in range(0, CHUNK, piece):
            at = slice(k, k + piece)
            e = jnp.exp2(split(s_s[kc, at]) * scale2 - m_new[None])
            s_s[kc, at] = e.reshape(piece, ROWS)
            est = e * split(st_s[kc, at])
            dp = split(dp_s[kc, at])
            z = z + jnp.sum(e, axis=0)
            s1 = s1 + jnp.sum(est, axis=0)
            d1 = d1 + jnp.sum(e * dp, axis=0)
            x1 = x1 + jnp.sum(est * dp, axis=0)
            y1 = y1 + jnp.sum(e * split(dpt_s[kc, at]), axis=0)
        for j, v in enumerate((m_new, z, s1, d1, x1, y1)):
            stats[t, j] = v

    def finish(t):
        m8, z, s1, d1, x1, y1 = [stats[t, j] for j in range(6)]
        top = jnp.max(m8, axis=0, keepdims=True)
        w8 = jnp.exp2(m8 - top)

        def total(v):
            return jnp.sum(v * w8, axis=0, keepdims=True)

        rz = 1.0 / total(z)
        tan_mean = total(s1) * rz
        delta = total(d1) * rz
        delta_tan = scaling * (total(x1) * rz - tan_mean * delta) + total(y1) * rz
        for j, v in enumerate((top, rz, tan_mean, delta, delta_tan)):
            stats[t, j] = jnp.broadcast_to(v, (8, ROWS))

    def grad_values(t, kc):
        s_s, st_s, dp_s, dpt_s = scores[t]
        top, rz, tan_mean, delta, delta_tan = [stats[t, j] for j in range(5)]
        f = jnp.exp2(mcs[t][kc] - top) * rz
        fc = f * scaling
        for k in range(0, CHUNK, piece):
            at = slice(k, k + piece)
            e = split(s_s[kc, at])
            p = e * f[None]
            pt = e * fc[None] * (split(st_s[kc, at]) - tan_mean[None])
            dd = split(dp_s[kc, at]) - delta[None]
            dst = pt * dd + p * (split(dpt_s[kc, at]) - delta_tan[None])
            for j, v in enumerate((dst, p * dd, pt)):
                xs[t][j, at] = v.reshape(piece, ROWS).astype(jnp.bfloat16)

    def grad_dots(i, group, kc):
        for t in group:
            x = xs[t][0:2].reshape(2 * CHUNK, ROWS)
            dqs[t][...] += dot(kts[kc], x, NN)
        left = jnp.concatenate([xs[t][j] for t in group for j in range(2)], axis=1)
        right = jnp.concatenate([qs[i, t, j] for t in group for j in range(2)], axis=0)
        dk = dot(left, right, NN)
        left = jnp.concatenate([xs[t][2] for t in group], axis=1)
        right = jnp.concatenate([qs[i, t, 2] for t in group], axis=0)
        dv = dot(left, right, NN)
        at = pl.ds(kc * per_chunk, per_chunk)
        acc[at, :, :HD] += dk.reshape(per_chunk, tokens, HD)
        acc[at, :, HD:] += dv.reshape(per_chunk, tokens, HD)

    def block(i, _):
        b = order_ref[jnp.where(i == 0, me, me ^ 1)]
        full = (b * tokens) // CHUNK
        stats[...] = jnp.zeros_like(stats)
        for t in range(tiles):
            stats[t, 0] = jnp.full((8, ROWS), FILL, jnp.float32)

        def score_step(kc, _, masked):
            score_dots(i, 0, kc, masked, b)
            for t in range(tiles):
                if t + 1 < tiles:
                    score_dots(i, t + 1, kc, masked, b)
                score_sums(t, kc)
            return 0

        lax.fori_loop(0, full, functools.partial(score_step, masked=False), 0)
        score_step(full, 0, True)
        for t in range(tiles):
            finish(t)
        for t in range(tiles):
            dqs[t][...] = jnp.zeros_like(dqs[t])

        def grad_step(kc, _):
            for at in range(0, tiles, span):
                for t in range(at, at + span):
                    grad_values(t, kc)
                if at:
                    grad_dots(i, range(at - span, at), kc)
            grad_dots(i, range(tiles - span, tiles), kc)
            return 0

        lax.fori_loop(0, full + 1, grad_step, 0)
        for t in range(tiles):
            dq = (dqs[t][...] * scaling).T.astype(jnp.bfloat16)
            wide = dq.astype(jnp.float32)
            sq_ref[...] += jnp.sum(split(wide * wide), axis=0)
            for h in range(per_tile):
                c = (t * per_tile + h) * HD
                dq_ref[i, :, c : c + HD] = dq[h * tokens : (h + 1) * tokens]
        return 0

    lax.fori_loop(0, 2, block, 0)

    for m, ref in enumerate(out_refs):
        for e in range(ref.shape[0] // tokens):
            block_at = acc[order_ref[out_seq(me, m, e)]]
            rows_at = slice(e * tokens, (e + 1) * tokens)
            ref[rows_at, :HD] = (block_at[:, :HD] * scaling).astype(ref.dtype)
            ref[rows_at, HD:] = block_at[:, HD:].astype(ref.dtype)


def run_hvp(me, order, q, qt, do, peer, own_kv, kvs, outs, seq_of, out_seq, col_of, width):
    tokens = q.shape[0]
    blocks = sum(k.shape[0] for k in kvs) + bool(own_kv)
    chunks = blocks * tokens // CHUNK
    tiles = width // ROWS
    f32 = jnp.float32
    score = pltpu.VMEM((chunks, CHUNK, ROWS), f32)
    kernel = functools.partial(
        hvp_kernel, seq_of, out_seq, len(own_kv), len(kvs), len(outs), tokens, width, col_of, HD ** (-0.5)
    )
    outs = [
        jax.ShapeDtypeStruct((2, tokens, width), jnp.bfloat16),
        jax.ShapeDtypeStruct((8, HD), f32),
    ] + outs
    flops = 2 * blocks * tokens * tokens * width * 10
    return pl.pallas_call(
        kernel,
        name="hvp",
        out_shape=outs,
        in_specs=[pl.BlockSpec(memory_space=pltpu.SMEM)]
        + [pl.BlockSpec(memory_space=pl.ANY)] * (5 + len(own_kv) + len(kvs)),
        out_specs=[pl.BlockSpec(memory_space=pltpu.VMEM)] * len(outs),
        scratch_shapes=[
            pltpu.VMEM((2, tiles, 3, ROWS, HD), jnp.bfloat16),
            pltpu.VMEM((blocks, tokens, 4 * HD), jnp.bfloat16),
            pltpu.VMEM((chunks, HD, 2 * CHUNK), jnp.bfloat16),
            pltpu.VMEM((blocks, tokens, 2 * HD), f32),
            pltpu.SemaphoreType.DMA((2,)),
            pltpu.VMEM((tiles, 6, 8, ROWS), f32),
            pltpu.SMEM(order.shape, jnp.int32),
        ]
        + [pltpu.VMEM((chunks, 8, ROWS), f32)] * tiles
        + [pltpu.VMEM((HD, ROWS), f32)] * tiles
        + [pltpu.VMEM((3, CHUNK, ROWS), jnp.bfloat16)] * tiles
        + [score] * (4 * tiles),
        compiler_params=pltpu.CompilerParams(vmem_limit_bytes=48 * 1024 * 1024),
        cost_estimate=pl.CostEstimate(flops=flops, bytes_accessed=4 << 20, transcendentals=0),
    )(me, order, q, qt, do, peer, *own_kv, *kvs)


def add_kernel(me_ref, own_ref, *rest):
    *got, dq_ref, dq_got_ref, sq_ref, dq_out, mine_ref, peer_ref, sum_ref, sem = rest
    width = dq_ref.shape[2]
    tokens = dq_ref.shape[1]
    core = lax.rem(me_ref[0], 2)
    mine = pl.multiple_of(core * width, HD)
    theirs = pl.multiple_of((1 - core) * width, HD)
    moves = (
        pltpu.make_async_copy(dq_ref.at[0], dq_out.at[:, pl.ds(mine, width)], sem.at[0]),
        pltpu.make_async_copy(dq_got_ref, dq_out.at[:, pl.ds(theirs, width)], sem.at[1]),
    )
    for move in moves:
        move.start()
    f32 = jnp.float32
    total = sq_ref[...]
    for e, out in enumerate((mine_ref, peer_ref)):
        rows = slice(e * tokens, (e + 1) * tokens)
        for cols in (slice(0, HD), slice(HD, 2 * HD)):
            final = own_ref[rows, cols]
            for ref in got:
                final = final + ref[rows, cols].astype(f32)
            final = final.astype(jnp.bfloat16)
            out[:, cols] = final
            wide = final.astype(f32)
            total = total + jnp.sum((wide * wide).reshape(-1, 8, HD), axis=0)
    line = jnp.sum(total, axis=0, keepdims=True)
    sum_ref[...] = jnp.broadcast_to(line[None], sum_ref.shape)
    for move in moves:
        move.wait()


def run_add(me, own, got, dq, dq_got, sq, devices):
    tokens, width = dq.shape[1:]
    half = jax.ShapeDtypeStruct((tokens, 2 * HD), jnp.bfloat16)
    return pl.pallas_call(
        add_kernel,
        name="add",
        out_shape=[
            jax.ShapeDtypeStruct((tokens, 2 * width), jnp.bfloat16),
            half,
            half,
            jax.ShapeDtypeStruct((devices, 1, HD), jnp.float32),
        ],
        in_specs=[pl.BlockSpec(memory_space=pltpu.SMEM)]
        + [pl.BlockSpec(memory_space=pltpu.VMEM)] * (len(got) + 4),
        out_specs=[pl.BlockSpec(memory_space=pl.ANY)]
        + [pl.BlockSpec(memory_space=pltpu.VMEM)] * 3,
        scratch_shapes=[pltpu.SemaphoreType.DMA((2,))],
        compiler_params=pltpu.CompilerParams(vmem_limit_bytes=4 << 20),
        cost_estimate=pl.CostEstimate(flops=1 << 20, bytes_accessed=2 << 20, transcendentals=0),
    )(me, own, *got, dq, dq_got, sq)


def pack_kernel(count, me_ref, *refs):
    core = lax.rem(me_ref[0], 2)
    sources, rows = refs[:count], refs[count:-4]
    theirs_ref, mine_ref, rows_ref, sem = refs[-4:]
    moves = []

    def move(ref, at, width, out, to):
        cols = pl.ds(pl.multiple_of(at * width, HD), width)
        moves.append(
            pltpu.make_async_copy(
                ref.at[:, cols], out.at[:, pl.ds(to * width, width)], sem.at[len(moves)]
            )
        )

    for out, head in ((theirs_ref, 1 - core), (mine_ref, core)):
        for j, ref in enumerate(sources):
            move(ref, head, HD, out, j)
    for j, ref in enumerate(rows):
        move(ref, 1 - core, ref.shape[1] // 2, rows_ref, j)
    for m in moves:
        m.start()
    for m in moves:
        m.wait()


def run_pack(me, sources, rows):
    tokens = rows[0].shape[0]
    half = jax.ShapeDtypeStruct((tokens, len(sources) * HD), sources[0].dtype)
    wide = jax.ShapeDtypeStruct((tokens, sum(r.shape[1] for r in rows) // 2), rows[0].dtype)
    count = 2 * len(sources) + len(rows)
    return pl.pallas_call(
        functools.partial(pack_kernel, len(sources)),
        name="pack",
        out_shape=[half, half, wide],
        in_specs=[pl.BlockSpec(memory_space=pltpu.SMEM)]
        + [pl.BlockSpec(memory_space=pltpu.HBM)] * (len(sources) + len(rows)),
        out_specs=[pl.BlockSpec(memory_space=pltpu.VMEM)] * 3,
        scratch_shapes=[pltpu.SemaphoreType.DMA((count,))],
        compiler_params=pltpu.CompilerParams(vmem_limit_bytes=60 * 1024 * 1024),
        cost_estimate=pl.CostEstimate(flops=1 << 16, bytes_accessed=1 << 21, transcendentals=0),
    )(me, *sources, *rows)


def last_kernel(me_ref, mine_ref, got_ref, lines_ref, dk_out, dv_out, norm_ref):
    core = lax.rem(me_ref[0], 2)
    for ref, at in ((mine_ref, core), (got_ref, 1 - core)):
        cols = pl.ds(pl.multiple_of(at * HD, HD), HD)
        dk_out[:, cols] = ref[:, :HD]
        dv_out[:, cols] = ref[:, HD:]
    norm_ref[0, 0] = jnp.sum(lines_ref[...])


def run_last(me, mine, got, lines):
    return pl.pallas_call(
        last_kernel,
        name="last",
        out_shape=[
            jax.ShapeDtypeStruct(mine.shape, mine.dtype),
            jax.ShapeDtypeStruct(mine.shape, mine.dtype),
            jax.ShapeDtypeStruct((1, 1), jnp.float32),
        ],
        in_specs=[pl.BlockSpec(memory_space=pltpu.SMEM)]
        + [pl.BlockSpec(memory_space=pltpu.VMEM)] * 3,
        out_specs=[pl.BlockSpec(memory_space=pltpu.VMEM)] * 2
        + [pl.BlockSpec(memory_space=pltpu.SMEM)],
        compiler_params=pltpu.CompilerParams(vmem_limit_bytes=4 << 20),
        cost_estimate=pl.CostEstimate(flops=1 << 16, bytes_accessed=1 << 18, transcendentals=0),
    )(me, mine, got, lines)


def shifted(x, axis, bit):
    size = lax.axis_size(axis)
    return lax.ppermute(x, axis, [(i, i ^ bit) for i in range(size)])


def all_sum(x, axes):
    for axis in axes:
        size = lax.axis_size(axis)
        if size & (size - 1):
            x = lax.psum(x, axis)
            continue
        bit = 1
        while bit < size:
            x = x + shifted(x, axis, bit)
            bit *= 2
    return x


def square_sum(x):
    w = x.astype(jnp.float32)
    return jnp.sum(w * w)


def join(core, mine, theirs):
    low = jnp.where(core == 0, mine, theirs)
    high = jnp.where(core == 0, theirs, mine)
    return jnp.concatenate([low, high], axis=1)


def body(queries, keys, values, q_tangent, k_tangent, v_tangent, out_grad, block_order):
    tokens = queries.shape[0]
    heads = keys.shape[1] // HD
    shards = lax.axis_size("seq")
    me = lax.axis_index("seq").astype(jnp.int32)
    core = lax.rem(me, 2)
    me_arr = me.reshape(1)
    width = heads * G * HD // 2
    other = (1 - core) * width
    f32 = jnp.float32

    def swap_rows(arrays):
        cut = [lax.dynamic_slice_in_dim(x, other, width, 1) for x in arrays]
        return shifted(jnp.concatenate(cut, axis=1), "seq", 1)

    rows = (queries, q_tangent, out_grad)

    def col_of(at):
        return lax.rem(at, 2) * width

    sources = (keys, k_tangent, values, v_tangent)


    if heads == 2 and shards == 8:
        theirs, mine, cut = run_pack(me_arr, sources, rows)
        peer_kv = shifted(theirs, "seq", 1)
        x_kv = [shifted(mine, "seq", 2), shifted(theirs, "seq", 3)]
        y_kv = [shifted(mine, "seq", 4), shifted(theirs, "seq", 5)]
        peer_rows = shifted(cut, "seq", 1)
        half = 2 * HD
        xy_a = shifted(jnp.stack([v[:, :half] for v in y_kv]), "seq", 2)
        xy_b = shifted(jnp.stack([v[:, half:] for v in x_kv]), "seq", 4)
        xy_kv = jnp.concatenate([xy_a, xy_b], axis=2)
        kvs = [v[None] for v in (peer_kv, *x_kv, *y_kv)] + [xy_kv]
        dq, sq, own, *parts = run_hvp(
            me_arr, block_order, *rows, peer_rows, sources, kvs,
            [jax.ShapeDtypeStruct((2 * tokens, 2 * HD), f32)]
            + [jax.ShapeDtypeStruct((2 * tokens, 2 * HD), jnp.bfloat16)] * (shards // 2 - 1),
            lambda at, m, e: at ^ (m + 1 + e), lambda at, m, e: at ^ (2 * m + e), col_of, width,
        )
        got = [shifted(p, "seq", 2 * m + 2) for m, p in enumerate(parts)]
        dq_got = shifted(dq[1], "seq", 1)
        devices = shards * lax.axis_size("head")
        dq_out, dkv_mine, dkv_peer, line = run_add(me_arr, own, got, dq, dq_got, sq, devices)
        dkv_got = shifted(dkv_peer, "seq", 1)
        lines = lax.all_to_all(line, ("head", "seq"), 0, 0)
        dk_out, dv_out, norm = run_last(me_arr, dkv_mine, dkv_got, lines)
        return (dq_out, dk_out, dv_out, norm[0, 0])
    assert heads == 1
    whole = lax.all_gather(jnp.concatenate(sources, axis=1), "seq", axis=0)
    dq, sq, parts = run_hvp(
        me_arr, block_order, *rows, swap_rows(rows), (), (whole,),
        [jax.ShapeDtypeStruct((shards * tokens, 2 * HD), jnp.bfloat16)],
        lambda at, m, e: e, lambda at, m, e: e, col_of, width,
    )
    final = lax.psum_scatter(parts, "seq", scatter_dimension=0, tiled=True)
    dq_out = join(core, dq[0], shifted(dq[1], "seq", 1))
    local = square_sum(final) + jnp.sum(sq)
    squared_norm = all_sum(local, ("seq", "head"))
    return (dq_out, final[:, :HD], final[:, HD:], squared_norm)


def solution(mesh):
    placed = (P("seq", "head"),) * 7 + (P(),)
    return jax.shard_map(
        body,
        mesh=mesh,
        in_specs=placed,
        out_specs=(P("seq", "head"), P("seq", "head"), P("seq", "head"), P()),
        check_vma=False,
    )
```

time: 70 us -> 57.9 us (0.83)
  starting transfers between devices: 19.8 us -> 13.1 us
  local copies, waits for them, and re-layouts: 3.87 us -> 0.65 us
  waiting for transfers between devices: 16.7 us -> 15.6 us
  other arithmetic: 0.77 us -> 0.05 us
    ppermute x14 -> x13, starting transfers between devices: 19.8 us -> 13.1 us  [shifted(): return lax.ppermute(x, axis, [(i, i ^ bit) for i in range(size)])]
    dynamic_slice x5 -> x0, local copies, waits for them, and re-layouts: 1.86 us -> none  [the longest x2 1.79 us: pack(): lax.dynamic_slice_in_dim(x, head * HD, HD, 1)]
    pallas_call x1, Pallas kernels: 12.7 us -> 11.3 us  [run_hvp(): pl.pallas_call(kernel, name='hvp', out_shape=outs, in_specs=[pl.BlockSpec...]
    unnamed x30 -> x16, local copies, waits for them, and re-layouts: 1.97 us -> 0.61 us
    ppermute x14 -> x13, waiting for transfers between devices: 16.7 us -> 15.6 us  [shifted(): return lax.ppermute(x, axis, [(i, i ^ bit) for i in range(size)])]
    pallas_call x1 -> x3, Pallas kernels: 2.83 us -> 3.89 us  [the longest x1 2.39 us: run_pack(): pl.pallas_call(functools.partial(pack_kernel, len(sources)), name='pack',...]
  transfers between devices with their start and end apart: 14 -> 13, of which waited for: 9 -> 6; matrix products, arithmetic and copies ran while one was open for 0% -> 0% of each run, Pallas kernels for 0% -> 0%
where the time goes in v1:
time: 57.9 us; the launch traced here: 57.7 us
  waiting for transfers between devices  15.6 us (27%)
  Pallas kernels  15.2 us (26%)
  starting transfers between devices  13.1 us (23%)
  blocking collectives  12.2 us (21%)
  between operations  0.87 us (2%)
  local copies, waits for them, and re-layouts  0.65 us (1%)
    ppermute x13, waiting for transfers between devices, shifted(): return lax.ppermute(x, axis, [(i, i ^ bit) for i in range(size)])  15.6 us
    ppermute x13, starting transfers between devices, shifted(): return lax.ppermute(x, axis, [(i, i ^ bit) for i in range(size)])  13.1 us
    all_to_all x1, blocking collectives, body(): lines = lax.all_to_all(line, ('head', 'seq'), 0, 0)  12.2 us
    pallas_call x1, Pallas kernels, run_hvp(): pl.pallas_call(kernel, name='hvp', out_shape=outs, in_specs=[pl.BlockSpec...  11.3 us
    pallas_call x1, Pallas kernels, run_pack(): pl.pallas_call(functools.partial(pack_kernel, len(sources)), name='pack',...  2.39 us
  transfers between devices with their start and end apart: 13, of which 6 were waited for; matrix products, arithmetic and copies ran while one was open for 0% of the time, Pallas kernels for 0%

profile of v1, /device:TPU:0, one launch (start us, length us, event | category | flops | bytes accessed | tf_op | source)
XLA Modules:
  0.0 57.7 jit_solution(6380571972358199648)
XLA Ops:
  0.6 0.0 copy-start.3
  0.6 0.0 copy-start.4
  0.7 0.0 copy-start.5
  0.7 0.0 copy-start.6
  0.7 2.4 %pack.1 = (bf16[128,512]{1,0:T(8,128)(2,1)}, bf16[128,512]{1,0:T(8,128)(2,1)}, bf16[128,3072]{1,0:T(8,128)(2,1)}) custom-call(s32[1]{0:T(128)} %bitcast.me_ref, bf16[128,256]{1,0:T(8,128)(2,1)} %rest_0_.1, bf16[128,256]{1,0:T(8,128)(2,1)} %rest_1_.1, bf16[128,256]{1,0:T(8,128)(2,1)} %rest_2_.1, bf16[128,256]{1,0:T(8,128)(2,1)} %rest_3_.1, ...), custom_call_target="tpu_custom_call" | custom-call | flops 65536 | bytes 2097152 | tf_op jit(solution)/shard_map/pack/pallas_call | solution.py:364
  3.1 3.1 %collective-permute-start.4 = (bf16[128,512]{1,0:T(8,128)(2,1)}, bf16[128,512]{1,0:T(8,128)(2,1)S(1)}, u32[]{:S(2)}, u32[]{:S(2)}) collective-permute-start(bf16[128,512]{1,0:T(8,128)(2,1)} %get-tuple-element.22), channel_id=1, source_target_pairs={{0,4},{1,5},{2,6},{3,7},{4,0},{5,1},{6,2},{7,3},{8,12},{9,13},{10,... | collective-permute-start | bytes 393224 | tf_op jit(solution)/shard_map/ppermute | solution.py:406
  6.1 1.5 %collective-permute-start.2 = (bf16[128,512]{1,0:T(8,128)(2,1)}, bf16[128,512]{1,0:T(8,128)(2,1)S(1)}, u32[]{:S(2)}, u32[]{:S(2)}) collective-permute-start(bf16[128,512]{1,0:T(8,128)(2,1)} %get-tuple-element.22), channel_id=1, source_target_pairs={{0,2},{1,3},{2,0},{3,1},{4,6},{5,7},{6,4},{7,5},{8,10},{9,11},{10,... | collective-permute-start | bytes 393224 | tf_op jit(solution)/shard_map/ppermute | solution.py:406
  7.6 0.0 collective-permute-start.5
  7.6 0.3 collective-permute-start.3
  8.0 0.3 collective-permute-start
  8.3 1.6 %collective-permute-done.4 = bf16[128,512]{1,0:T(8,128)(2,1)S(1)} collective-permute-done((bf16[128,512]{1,0:T(8,128)(2,1)}, bf16[128,512]{1,0:T(8,128)(2,1)S(1)}, u32[]{:S(2)}, u32[]{:S(2)}) %collective-permute-start.4) | collective-permute-done | bytes 131104 | tf_op jit(solution)/shard_map/ppermute | solution.py:406
  9.8 0.0 copy-start.2
  9.8 3.2 %collective-permute-done.5 = bf16[128,512]{1,0:T(8,128)(2,1)S(1)} collective-permute-done((bf16[128,512]{1,0:T(8,128)(2,1)}, bf16[128,512]{1,0:T(8,128)(2,1)S(1)}, u32[]{:S(2)}, u32[]{:S(2)}) %collective-permute-start.5) | collective-permute-done | bytes 131104 | tf_op jit(solution)/shard_map/ppermute | solution.py:406
  13.1 0.0 copy-start
  13.1 0.0 copy-start.1
  13.1 1.1 %collective-permute-start.6 = (bf16[2,128,256]{2,1,0:T(8,128)(2,1)S(1)}, bf16[2,128,256]{2,1,0:T(8,128)(2,1)S(1)}, u32[]{:S(2)}, u32[]{:S(2)}) collective-permute-start(bf16[2,128,256]{2,1,0:T(8,128)(2,1)S(1)} %pad_maximum_fusion.1), channel_id=1, source_target_pairs={{0,2},{1,3},{2,0},{3,1},{4,6},{5,7},{6,4},{7,5},{8,10},{9,11},{10,... | collective-permute-start | bytes 393224 | tf_op jit(solution)/shard_map/ppermute | solution.py:406
  14.3 0.0 collective-permute-done.2
  14.3 0.0 collective-permute-done.3
  14.3 0.6 %collective-permute-start.7 = (bf16[2,128,256]{2,1,0:T(8,128)(2,1)S(1)}, bf16[2,128,256]{2,1,0:T(8,128)(2,1)S(1)}, u32[]{:S(2)}, u32[]{:S(2)}) collective-permute-start(bf16[2,128,256]{2,1,0:T(8,128)(2,1)S(1)} %pad_maximum_fusion.2), channel_id=1, source_target_pairs={{0,4},{1,5},{2,6},{3,7},{4,0},{5,1},{6,2},{7,3},{8,12},{9,13},{10,... | collective-permute-start | bytes 393224 | tf_op jit(solution)/shard_map/ppermute | solution.py:406
  15.0 0.5 collective-permute-start.1
  15.5 2.7 %collective-permute-done.6 = bf16[2,128,256]{2,1,0:T(8,128)(2,1)S(1)} collective-permute-done((bf16[2,128,256]{2,1,0:T(8,128)(2,1)S(1)}, bf16[2,128,256]{2,1,0:T(8,128)(2,1)S(1)}, u32[]{:S(2)}, u32[]{:S(2)}) %collective-permute-start.6) | collective-permute-done | bytes 131104 | tf_op jit(solution)/shard_map/ppermute | solution.py:406
  18.2 1.5 %collective-permute-done.7 = bf16[2,128,256]{2,1,0:T(8,128)(2,1)S(1)} collective-permute-done((bf16[2,128,256]{2,1,0:T(8,128)(2,1)S(1)}, bf16[2,128,256]{2,1,0:T(8,128)(2,1)S(1)}, u32[]{:S(2)}, u32[]{:S(2)}) %collective-permute-start.7) | collective-permute-done | bytes 131104 | tf_op jit(solution)/shard_map/ppermute | solution.py:406
  19.7 0.0 collective-permute-done.1
  19.7 0.0 collective-permute-done.peer_ref
  19.7 0.0 copy-start.7
  19.7 0.0 copy-done.3
  19.7 0.0 copy-done.4
  19.7 0.0 copy-done.5
  19.8 0.0 copy-done.6
  19.8 0.0 copy-done.2
  19.8 0.0 copy-done
  19.8 0.0 copy-done.1
  19.8 0.6 copy-done.7
  20.4 11.3 %hvp.1 = (bf16[2,128,1024]{2,1,0:T(8,128)(2,1)S(1)}, f32[8,128]{1,0:T(8,128)S(1)}, f32[256,256]{1,0:T(8,128)S(1)}, bf16[256,256]{1,0:T(8,128)(2,1)S(1)}, bf16[25...) custom-call(s32[1]{0:T(128)} %bitcast.me_ref, s32[8]{0:T(128)S(1)} %copy-done.7, bf16[128,2048]{1,0:T(8,128)(2,1)S(1)} %copy-done, ...), custom_call_target="tpu_custom_call" | custom-call | flops 2684354560 | bytes 4194304 | tf_op jit(solution)/shard_map/hvp/pallas_call | solution.py:256
  31.7 0.1 collective-permute-start.11
  31.8 0.1 collective-permute-start.8
  31.9 5.4 %collective-permute-start.9 = (bf16[256,256]{1,0:T(8,128)(2,1)S(1)}, bf16[256,256]{1,0:T(8,128)(2,1)S(1)}, u32[]{:S(2)}, u32[]{:S(2)}) collective-permute-start(bf16[256,256]{1,0:T(8,128)(2,1)S(1)} %get-tuple-element.25), channel_id=1, source_target_pairs={{0,4},{1,5},{2,6},{3,7},{4,0},{5,1},{6,2},{7,3},{8,12},{9,13},{10,... | collective-permute-start | bytes 393224 | tf_op jit(solution)/shard_map/ppermute | solution.py:406
  37.3 0.0 collective-permute-start.10
  37.3 0.5 collective-permute-done.8.rest_0_
  37.7 6.2 %collective-permute-done.9.rest_1_ = bf16[256,256]{1,0:T(8,128)(2,1)S(1)} collective-permute-done((bf16[256,256]{1,0:T(8,128)(2,1)S(1)}, bf16[256,256]{1,0:T(8,128)(2,1)S(1)}, u32[]{:S(2)}, u32[]{:S(2)}) %collective-permute-start.9) | collective-permute-done | bytes 131104 | tf_op jit(solution)/shard_map/ppermute | solution.py:406
  43.9 0.0 collective-permute-done.10.rest_2_
  43.9 0.0 collective-permute-done.11.rest_4_
  43.9 0.8 %add.1 = (bf16[128,2048]{1,0:T(8,128)(2,1)}, bf16[128,256]{1,0:T(8,128)(2,1)S(1)}, bf16[128,256]{1,0:T(8,128)(2,1)S(1)}, f32[32,1,128]{2,1,0:T(1,128)S(1)}) custom-call(s32[1]{0:T(128)} %bitcast.me_ref, f32[256,256]{1,0:T(8,128)S(1)} %get-tuple-element.23.own_ref, bf16[256,256]{1,0:T(8,128)(2,1)S(1)} %collective-permute-done.8.rest_0_, ...), custom_call_target="tpu_custom_call" | custom-call | flops 1048576 | bytes 2097152 | tf_op jit(solution)/shard_map/add/pallas_call | solution.py:315
  44.7 0.1 collective-permute-start.12
  44.8 12.2 %all_to_all.5.lines_ref = f32[32,1,128]{2,1,0:T(1,128)S(1)} all-to-all(f32[32,1,128]{2,1,0:T(1,128)S(1)} %get-tuple-element.32), channel_id=1, replica_groups=mesh['head'=4,'seq'=8] {'head','seq'}, dimensions={0} | all-to-all | bytes 32768 | tf_op jit(solution)/shard_map/all_to_all | solution.py:478
  57.0 0.0 collective-permute-done.12.got_ref
  57.0 0.7 %last.1 = (bf16[128,256]{1,0:T(8,128)(2,1)}, bf16[128,256]{1,0:T(8,128)(2,1)}, f32[1,1]{1,0:T(1,128)}) custom-call(s32[1]{0:T(128)} %bitcast.me_ref, bf16[128,256]{1,0:T(8,128)(2,1)S(1)} %get-tuple-element.30.mine_ref, bf16[128,256]{1,0:T(8,128)(2,1)S(1)} %collective-permute-done.12.got_ref, f32[32,1,128]{2,1,0:T(1,128)S(1)} %all_to_all.5.lines_ref), custom_call_target="tpu_custom_call" | custom-call | flops 65536 | bytes 262144 | tf_op jit(solution)/shard_map/last/pallas_call | solution.py:387
  (8 shorter events, 0.1 us)
Async XLA Ops:
  0.6 19.1 %copy-start.3 = (bf16[128,256]{1,0:T(8,128)(2,1)S(1)}, bf16[128,256]{1,0:T(8,128)(2,1)}, u32[]{:S(2)}) copy-start(bf16[128,256]{1,0:T(8,128)(2,1)} %rest_0_.1) | copy-start | bytes 196612
  0.6 19.1 %copy-start.4 = (bf16[128,256]{1,0:T(8,128)(2,1)S(1)}, bf16[128,256]{1,0:T(8,128)(2,1)}, u32[]{:S(2)}) copy-start(bf16[128,256]{1,0:T(8,128)(2,1)} %rest_1_.1) | copy-start | bytes 196612
  0.7 19.1 %copy-start.5 = (bf16[128,256]{1,0:T(8,128)(2,1)S(1)}, bf16[128,256]{1,0:T(8,128)(2,1)}, u32[]{:S(2)}) copy-start(bf16[128,256]{1,0:T(8,128)(2,1)} %rest_2_.1) | copy-start | bytes 196612
  0.7 19.1 %copy-start.6 = (bf16[128,256]{1,0:T(8,128)(2,1)S(1)}, bf16[128,256]{1,0:T(8,128)(2,1)}, u32[]{:S(2)}) copy-start(bf16[128,256]{1,0:T(8,128)(2,1)} %rest_3_.1) | copy-start | bytes 196612
  3.1 6.8 %collective-permute-start.4 = (bf16[128,512]{1,0:T(8,128)(2,1)}, bf16[128,512]{1,0:T(8,128)(2,1)S(1)}, u32[]{:S(2)}, u32[]{:S(2)}) collective-permute-start(bf16[128,512]{1,0:T(8,128)(2,1)} %get-tuple-element.22), channel_id=1, source_target_pairs={{0,4},{1,5},{2,6},{3,7},{4,0},{5,1},{6,2},{7,3},{8,12},{9,13},{10,... | collective-permute-start | bytes 393224 | tf_op jit(solution)/shard_map/ppermute | solution.py:406
  6.1 8.1 %collective-permute-start.2 = (bf16[128,512]{1,0:T(8,128)(2,1)}, bf16[128,512]{1,0:T(8,128)(2,1)S(1)}, u32[]{:S(2)}, u32[]{:S(2)}) collective-permute-start(bf16[128,512]{1,0:T(8,128)(2,1)} %get-tuple-element.22), channel_id=1, source_target_pairs={{0,2},{1,3},{2,0},{3,1},{4,6},{5,7},{6,4},{7,5},{8,10},{9,11},{10,... | collective-permute-start | bytes 393224 | tf_op jit(solution)/shard_map/ppermute | solution.py:406
  7.6 5.5 %collective-permute-start.5 = (bf16[128,512]{1,0:T(8,128)(2,1)}, bf16[128,512]{1,0:T(8,128)(2,1)S(1)}, u32[]{:S(2)}, u32[]{:S(2)}) collective-permute-start(bf16[128,512]{1,0:T(8,128)(2,1)} %get-tuple-element.21), channel_id=1, source_target_pairs={{0,5},{1,4},{2,7},{3,6},{4,1},{5,0},{6,3},{7,2},{8,13},{9,12},{10,... | collective-permute-start | bytes 393224 | tf_op jit(solution)/shard_map/ppermute | solution.py:406
  7.6 6.7 %collective-permute-start.3 = (bf16[128,512]{1,0:T(8,128)(2,1)}, bf16[128,512]{1,0:T(8,128)(2,1)S(1)}, u32[]{:S(2)}, u32[]{:S(2)}) collective-permute-start(bf16[128,512]{1,0:T(8,128)(2,1)} %get-tuple-element.21), channel_id=1, source_target_pairs={{0,3},{1,2},{2,1},{3,0},{4,7},{5,6},{6,5},{7,4},{8,11},{9,10},{10,... | collective-permute-start | bytes 393224 | tf_op jit(solution)/shard_map/ppermute | solution.py:406
  8.0 11.7 %collective-permute-start = (bf16[128,3072]{1,0:T(8,128)(2,1)}, bf16[128,3072]{1,0:T(8,128)(2,1)S(1)}, u32[]{:S(2)}, u32[]{:S(2)}) collective-permute-start(bf16[128,3072]{1,0:T(8,128)(2,1)} %get-tuple-element.20), channel_id=1, source_target_pairs={{0,1},{1,0},{2,3},{3,2},{4,5},{5,4},{6,7},{7,6},{8,9},{9,8},{10,11... | collective-permute-start | bytes 2359304 | tf_op jit(solution)/shard_map/ppermute | solution.py:406
  9.8 9.9 %copy-start.2 = (bf16[128,2048]{1,0:T(8,128)(2,1)S(1)}, bf16[128,2048]{1,0:T(8,128)(2,1)}, u32[]{:S(2)}) copy-start(bf16[128,2048]{1,0:T(8,128)(2,1)} %do_ref.1) | copy-start | bytes 1572868
  13.1 6.7 %copy-start = (bf16[128,2048]{1,0:T(8,128)(2,1)S(1)}, bf16[128,2048]{1,0:T(8,128)(2,1)}, u32[]{:S(2)}) copy-start(bf16[128,2048]{1,0:T(8,128)(2,1)} %q_ref.1) | copy-start | bytes 1572868
  13.1 6.7 %copy-start.1 = (bf16[128,2048]{1,0:T(8,128)(2,1)S(1)}, bf16[128,2048]{1,0:T(8,128)(2,1)}, u32[]{:S(2)}) copy-start(bf16[128,2048]{1,0:T(8,128)(2,1)} %qt_ref.1) | copy-start | bytes 1572868
  13.1 5.0 %collective-permute-start.6 = (bf16[2,128,256]{2,1,0:T(8,128)(2,1)S(1)}, bf16[2,128,256]{2,1,0:T(8,128)(2,1)S(1)}, u32[]{:S(2)}, u32[]{:S(2)}) collective-permute-start(bf16[2,128,256]{2,1,0:T(8,128)(2,1)S(1)} %pad_maximum_fusion.1), channel_id=1, source_target_pairs={{0,2},{1,3},{2,0},{3,1},{4,6},{5,7},{6,4},{7,5},{8,10},{9,11},{10,... | collective-permute-start | bytes 393224 | tf_op jit(solution)/shard_map/ppermute | solution.py:406
  14.3 5.3 %collective-permute-start.7 = (bf16[2,128,256]{2,1,0:T(8,128)(2,1)S(1)}, bf16[2,128,256]{2,1,0:T(8,128)(2,1)S(1)}, u32[]{:S(2)}, u32[]{:S(2)}) collective-permute-start(bf16[2,128,256]{2,1,0:T(8,128)(2,1)S(1)} %pad_maximum_fusion.2), channel_id=1, source_target_pairs={{0,4},{1,5},{2,6},{3,7},{4,0},{5,1},{6,2},{7,3},{8,12},{9,13},{10,... | collective-permute-start | bytes 393224 | tf_op jit(solution)/shard_map/ppermute | solution.py:406
  15.0 4.7 %collective-permute-start.1 = (bf16[128,512]{1,0:T(8,128)(2,1)}, bf16[128,512]{1,0:T(8,128)(2,1)S(1)}, u32[]{:S(2)}, u32[]{:S(2)}) collective-permute-start(bf16[128,512]{1,0:T(8,128)(2,1)} %get-tuple-element.21), channel_id=1, source_target_pairs={{0,1},{1,0},{2,3},{3,2},{4,5},{5,4},{6,7},{7,6},{8,9},{9,8},{10,11... | collective-permute-start | bytes 393224 | tf_op jit(solution)/shard_map/ppermute | solution.py:406
  19.7 0.7 %copy-start.7 = (s32[8]{0:T(128)S(1)}, s32[8]{0:T(128)}, u32[]{:S(2)}) copy-start(s32[8]{0:T(128)} %order_hbm.1) | copy-start | bytes 100
  31.7 12.1 %collective-permute-start.11 = (bf16[128,1024]{1,0:T(8,128)(2,1)S(1)}, bf16[128,1024]{1,0:T(8,128)(2,1)S(1)}, u32[]{:S(2)}, u32[]{:S(2)}) collective-permute-start(bf16[128,1024]{1,0:T(8,128)(2,1)S(1)} %slice_bitcast_fusion), channel_id=1, source_target_pairs={{0,1},{1,0},{2,3},{3,2},{4,5},{5,4},{6,7},{7,6},{8,9},{9,8},{10,11... | collective-permute-start | bytes 786440 | tf_op jit(solution)/shard_map/ppermute | solution.py:406
  31.8 5.9 %collective-permute-start.8 = (bf16[256,256]{1,0:T(8,128)(2,1)S(1)}, bf16[256,256]{1,0:T(8,128)(2,1)S(1)}, u32[]{:S(2)}, u32[]{:S(2)}) collective-permute-start(bf16[256,256]{1,0:T(8,128)(2,1)S(1)} %get-tuple-element.24), channel_id=1, source_target_pairs={{0,2},{1,3},{2,0},{3,1},{4,6},{5,7},{6,4},{7,5},{8,10},{9,11},{10,... | collective-permute-start | bytes 393224 | tf_op jit(solution)/shard_map/ppermute | solution.py:406
  31.9 12.0 %collective-permute-start.9 = (bf16[256,256]{1,0:T(8,128)(2,1)S(1)}, bf16[256,256]{1,0:T(8,128)(2,1)S(1)}, u32[]{:S(2)}, u32[]{:S(2)}) collective-permute-start(bf16[256,256]{1,0:T(8,128)(2,1)S(1)} %get-tuple-element.25), channel_id=1, source_target_pairs={{0,4},{1,5},{2,6},{3,7},{4,0},{5,1},{6,2},{7,3},{8,12},{9,13},{10,... | collective-permute-start | bytes 393224 | tf_op jit(solution)/shard_map/ppermute | solution.py:406
  37.3 6.6 %collective-permute-start.10 = (bf16[256,256]{1,0:T(8,128)(2,1)S(1)}, bf16[256,256]{1,0:T(8,128)(2,1)S(1)}, u32[]{:S(2)}, u32[]{:S(2)}) collective-permute-start(bf16[256,256]{1,0:T(8,128)(2,1)S(1)} %get-tuple-element.26), channel_id=1, source_target_pairs={{0,6},{1,7},{2,4},{3,5},{4,2},{5,3},{6,0},{7,1},{8,14},{9,15},{10,... | collective-permute-start | bytes 393224 | tf_op jit(solution)/shard_map/ppermute | solution.py:406
  44.7 12.3 %collective-permute-start.12 = (bf16[128,256]{1,0:T(8,128)(2,1)S(1)}, bf16[128,256]{1,0:T(8,128)(2,1)S(1)}, u32[]{:S(2)}, u32[]{:S(2)}) collective-permute-start(bf16[128,256]{1,0:T(8,128)(2,1)S(1)} %get-tuple-element.31), channel_id=1, source_target_pairs={{0,1},{1,0},{2,3},{3,2},{4,5},{5,4},{6,7},{7,6},{8,9},{9,8},{10,11... | collective-permute-start | bytes 196616 | tf_op jit(solution)/shard_map/ppermute | solution.py:406

commit v2 on v1

--- a/solution.py
+++ b/solution.py
@@ -33,9 +33,15 @@
     rest = rest[n_kv + 2 + n_out :]
     groups = width // HD
     tiles = width // ROWS
-    qs, kvs, kts, acc, sem, stats, order_ref = rest[:7]
-    mcs, dqs, xs = (rest[7 + j * tiles : 7 + (j + 1) * tiles] for j in range(3))
-    scores = [rest[7 + 3 * tiles + 4 * t :][:4] for t in range(tiles)]
+    qs, kvs, kts, acc, sem, order_ref = rest[:6]
+    rest = rest[6:]
+    dqs, xs, rest = rest[:tiles], rest[tiles : 2 * tiles], rest[2 * tiles :]
+    held = 5 * tiles + 1
+    sets = len(rest) // held
+    rest = [rest[w * held : (w + 1) * held] for w in range(sets)] * (3 - sets)
+    stats_sets = [r[0] for r in rest]
+    mcs = [r[1 : 1 + tiles] for r in rest]
+    scores = [[r[1 + tiles + 4 * t :][:4] for t in range(tiles)] for r in rest]
     per_tile = ROWS // tokens
     me = me_ref[0]
     first = col_of(me)
@@ -104,8 +110,8 @@
     piece = 32
     span = min(1, tiles)
 
-    def score_dots(i, t, kc, masked, b):
-        s_s, st_s, dp_s, dpt_s = scores[t]
+    def score_dots(w, i, t, kc, masked, b):
+        s_s, st_s, dp_s, dpt_s = scores[w][t]
         q, qt, do = qs[i, t, 0], qs[i, t, 1], qs[i, t, 2]
         kv = chunk_kv(kc)
         s = dot(kv[:, :HD], q, NT)
@@ -119,15 +125,16 @@
         dp_s[kc] = both[:CHUNK]
         dpt_s[kc] = both[CHUNK:]
 
-    def score_sums(t, kc):
-        s_s, st_s, dp_s, dpt_s = scores[t]
+    def score_sums(w, t, kc):
+        s_s, st_s, dp_s, dpt_s = scores[w][t]
+        stats = stats_sets[w]
         m_old, z, s1, d1, x1, y1 = [stats[t, j] for j in range(6)]
         m_new = m_old
         for k in range(0, CHUNK, piece):
             s = split(s_s[kc, k : k + piece])
             m_new = jnp.maximum(m_new, jnp.max(s, axis=0) * scale2)
         decay = jnp.exp2(m_old - m_new)
-        mcs[t][kc] = m_new
+        mcs[w][t][kc] = m_new
         z, s1, d1, x1, y1 = [v * decay for v in (z, s1, d1, x1, y1)]
         for k in range(0, CHUNK, piece):
             at = slice(k, k + piece)
@@ -143,7 +150,8 @@
         for j, v in enumerate((m_new, z, s1, d1, x1, y1)):
             stats[t, j] = v
 
-    def finish(t):
+    def finish(w, t):
+        stats = stats_sets[w]
         m8, z, s1, d1, x1, y1 = [stats[t, j] for j in range(6)]
         top = jnp.max(m8, axis=0, keepdims=True)
         w8 = jnp.exp2(m8 - top)
@@ -158,10 +166,11 @@
         for j, v in enumerate((top, rz, tan_mean, delta, delta_tan)):
             stats[t, j] = jnp.broadcast_to(v, (8, ROWS))
 
-    def grad_values(t, kc):
-        s_s, st_s, dp_s, dpt_s = scores[t]
+    def grad_values(w, t, kc):
+        s_s, st_s, dp_s, dpt_s = scores[w][t]
+        stats = stats_sets[w]
         top, rz, tan_mean, delta, delta_tan = [stats[t, j] for j in range(5)]
-        f = jnp.exp2(mcs[t][kc] - top) * rz
+        f = jnp.exp2(mcs[w][t][kc] - top) * rz
         fc = f * scaling
         for k in range(0, CHUNK, piece):
             at = slice(k, k + piece)
@@ -187,38 +196,38 @@
         acc[at, :, :HD] += dk.reshape(per_chunk, tokens, HD)
         acc[at, :, HD:] += dv.reshape(per_chunk, tokens, HD)
 
-    def block(i, _):
-        b = order_ref[jnp.where(i == 0, me, me ^ 1)]
-        full = (b * tokens) // CHUNK
-        stats[...] = jnp.zeros_like(stats)
+    def score_step(kc, _, w, i, b, masked):
+        score_dots(w, i, 0, kc, masked, b)
         for t in range(tiles):
-            stats[t, 0] = jnp.full((8, ROWS), FILL, jnp.float32)
-
-        def score_step(kc, _, masked):
-            score_dots(i, 0, kc, masked, b)
-            for t in range(tiles):
-                if t + 1 < tiles:
-                    score_dots(i, t + 1, kc, masked, b)
-                score_sums(t, kc)
-            return 0
-
-        lax.fori_loop(0, full, functools.partial(score_step, masked=False), 0)
-        score_step(full, 0, True)
+            if t + 1 < tiles:
+                score_dots(w, i, t + 1, kc, masked, b)
+            score_sums(w, t, kc)
+        return 0
+
+    def grad_step(kc, _, w, i):
         for t in range(tiles):
-            finish(t)
+            grad_values(w, t, kc)
+            grad_dots(i, (t,), kc)
+        return 0
+
+    def both_step(kc, _):
+        for t in range(tiles):
+            score_dots(1, i1, t, kc, False, b1)
+            grad_values(0, t, kc)
+            grad_dots(i0, (t,), kc)
+            score_sums(1, t, kc)
+        return 0
+
+    def clear(w):
+        stats_sets[w][...] = jnp.zeros_like(stats_sets[w])
+        for t in range(tiles):
+            stats_sets[w][t, 0] = jnp.full((8, ROWS), FILL, jnp.float32)
+
+    def clear_dq():
         for t in range(tiles):
             dqs[t][...] = jnp.zeros_like(dqs[t])
 
-        def grad_step(kc, _):
-            for at in range(0, tiles, span):
-                for t in range(at, at + span):
-                    grad_values(t, kc)
-                if at:
-                    grad_dots(i, range(at - span, at), kc)
-            grad_dots(i, range(tiles - span, tiles), kc)
-            return 0
-
-        lax.fori_loop(0, full + 1, grad_step, 0)
+    def store_dq(i):
         for t in range(tiles):
             dq = (dqs[t][...] * scaling).T.astype(jnp.bfloat16)
             wide = dq.astype(jnp.float32)
@@ -226,9 +235,37 @@
             for h in range(per_tile):
                 c = (t * per_tile + h) * HD
                 dq_ref[i, :, c : c + HD] = dq[h * tokens : (h + 1) * tokens]
-        return 0
-
-    lax.fori_loop(0, 2, block, 0)
+
+    def run(low, high, step, **fixed):
+        lax.fori_loop(low, high, functools.partial(step, **fixed), 0)
+
+    own, peer = order_ref[me], order_ref[me ^ 1]
+    i0 = (own > peer).astype(jnp.int32)
+    i1 = 1 - i0
+    b0, b1 = jnp.minimum(own, peer), jnp.maximum(own, peer)
+    full0, full1 = (b0 * tokens) // CHUNK, (b1 * tokens) // CHUNK
+    clear(0)
+    run(0, full0, score_step, w=0, i=i0, b=b0, masked=False)
+    score_step(full0, 0, 0, i0, b0, True)
+    for t in range(tiles):
+        finish(0, t)
+    clear_dq()
+    joint = 0
+    if sets > 1:
+        clear(1)
+        joint = jnp.minimum(full0 + 1, full1)
+        run(0, joint, both_step)
+    run(joint, full0 + 1, grad_step, w=0, i=i0)
+    store_dq(i0)
+    clear_dq()
+    if sets == 1:
+        clear(1)
+    run(joint, full1, score_step, w=1, i=i1, b=b1, masked=False)
+    score_step(full1, 0, 1, i1, b1, True)
+    for t in range(tiles):
+        finish(1, t)
+    run(0, full1 + 1, grad_step, w=1, i=i1)
+    store_dq(i1)
 
     for m, ref in enumerate(out_refs):
         for e in range(ref.shape[0] // tokens):
@@ -245,6 +282,7 @@
     tiles = width // ROWS
     f32 = jnp.float32
     score = pltpu.VMEM((chunks, CHUNK, ROWS), f32)
+    sets = 2 if 2 * 4 * tiles * chunks * CHUNK * ROWS * 4 <= 36 << 20 else 1
     kernel = functools.partial(
         hvp_kernel, seq_of, out_seq, len(own_kv), len(kvs), len(outs), tokens, width, col_of, HD ** (-0.5)
     )
@@ -266,16 +304,19 @@
             pltpu.VMEM((chunks, HD, 2 * CHUNK), jnp.bfloat16),
             pltpu.VMEM((blocks, tokens, 2 * HD), f32),
             pltpu.SemaphoreType.DMA((2,)),
-            pltpu.VMEM((tiles, 6, 8, ROWS), f32),
             pltpu.SMEM(order.shape, jnp.int32),
         ]
-        + [pltpu.VMEM((chunks, 8, ROWS), f32)] * tiles
         + [pltpu.VMEM((HD, ROWS), f32)] * tiles
         + [pltpu.VMEM((3, CHUNK, ROWS), jnp.bfloat16)] * tiles
-        + [score] * (4 * tiles),
+        + sets
+        * (
+            [pltpu.VMEM((tiles, 6, 8, ROWS), f32)]
+            + [pltpu.VMEM((chunks, 8, ROWS), f32)] * tiles
+            + [score] * (4 * tiles)
+        ),
         compiler_params=pltpu.CompilerParams(vmem_limit_bytes=48 * 1024 * 1024),
         cost_estimate=pl.CostEstimate(flops=flops, bytes_accessed=4 << 20, transcendentals=0),
-    )(me, order, q, qt, do, peer, *own_kv, *kvs)
+    )(me, in_hbm(order), q, qt, do, peer, *own_kv, *kvs)
 
 
 def add_kernel(me_ref, own_ref, *rest):
@@ -331,6 +372,10 @@
     )(me, own, *got, dq, dq_got, sq)
 
 
+def in_hbm(x):
+    return pltpu.with_memory_space_constraint(x, pltpu.HBM)
+
+
 def pack_kernel(count, me_ref, *refs):
     core = lax.rem(me_ref[0], 2)
     sources, rows = refs[:count], refs[count:-4]
@@ -358,8 +403,8 @@
 
 def run_pack(me, sources, rows):
     tokens = rows[0].shape[0]
-    half = jax.ShapeDtypeStruct((tokens, len(sources) * HD), sources[0].dtype)
-    wide = jax.ShapeDtypeStruct((tokens, sum(r.shape[1] for r in rows) // 2), rows[0].dtype)
+    half = pltpu.VMEM((tokens, len(sources) * HD), sources[0].dtype)
+    wide = pltpu.VMEM((tokens, sum(r.shape[1] for r in rows) // 2), rows[0].dtype)
     count = 2 * len(sources) + len(rows)
     return pl.pallas_call(
         functools.partial(pack_kernel, len(sources)),
@@ -369,9 +414,9 @@
         + [pl.BlockSpec(memory_space=pltpu.HBM)] * (len(sources) + len(rows)),
         out_specs=[pl.BlockSpec(memory_space=pltpu.VMEM)] * 3,
         scratch_shapes=[pltpu.SemaphoreType.DMA((count,))],
-        compiler_params=pltpu.CompilerParams(vmem_limit_bytes=60 * 1024 * 1024),
+        compiler_params=pltpu.CompilerParams(vmem_limit_bytes=4 << 20),
         cost_estimate=pl.CostEstimate(flops=1 << 16, bytes_accessed=1 << 21, transcendentals=0),
-    )(me, *sources, *rows)
+    )(me, *map(in_hbm, sources), *map(in_hbm, rows))
 
 
 def last_kernel(me_ref, mine_ref, got_ref, lines_ref, dk_out, dv_out, norm_ref):

time: 57.9 us -> 56.3 us (0.972); the launches traced: 57.7 us -> 55.2 us
  Pallas kernels: 15.2 us -> 12.7 us
  starting transfers between devices: 13.1 us -> 13.9 us
  local copies, waits for them, and re-layouts: 0.65 us -> 0.07 us
    pallas_call x1, Pallas kernels: 11.3 us -> 9.74 us  [run_hvp(): pl.pallas_call(kernel, name='hvp', out_shape=outs, in_specs=[pl.BlockSpec...]
    pallas_call x1, Pallas kernels: 2.39 us -> 1.43 us  [run_pack(): pl.pallas_call(functools.partial(pack_kernel, len(sources)), name='pack',...]
    ppermute x13, starting transfers between devices: 13.1 us -> 13.9 us  [shifted(): return lax.ppermute(x, axis, [(i, i ^ bit) for i in range(size)])]
    unnamed x16 -> x14, local copies, waits for them, and re-layouts: 0.61 us -> 0.03 us
  transfers between devices with their start and end apart: 13 -> 13, of which waited for: 6 -> 7; matrix products, arithmetic and copies ran while one was open for 0% -> 0% of each run, Pallas kernels for 0% -> 0%
where the time goes in v2:
time: 56.3 us; the launch traced here: 55.2 us
  waiting for transfers between devices  15.4 us (27%)
  starting transfers between devices  13.9 us (25%)
  Pallas kernels  12.7 us (23%)
  blocking collectives  12.2 us (22%)
  between operations  0.85 us (2%)
    ppermute x13, waiting for transfers between devices, shifted(): return lax.ppermute(x, axis, [(i, i ^ bit) for i in range(size)])  15.4 us
    ppermute x13, starting transfers between devices, shifted(): return lax.ppermute(x, axis, [(i, i ^ bit) for i in range(size)])  13.9 us
    all_to_all x1, blocking collectives, body(): lines = lax.all_to_all(line, ('head', 'seq'), 0, 0)  12.2 us
    pallas_call x1, Pallas kernels, run_hvp(): pl.pallas_call(kernel, name='hvp', out_shape=outs, in_specs=[pl.BlockSpec...  9.74 us
    pallas_call x1, Pallas kernels, run_pack(): pl.pallas_call(functools.partial(pack_kernel, len(sources)), name='pack',...  1.43 us
  transfers between devices with their start and end apart: 13, of which 7 were waited for; matrix products, arithmetic and copies ran while one was open for 0% of the time, Pallas kernels for 0%

profile of v2, /device:TPU:0, one launch (start us, length us, event | category | flops | bytes accessed | tf_op | source)
XLA Modules:
  0.0 55.2 jit_solution(17718315951274494720)
XLA Ops:
  0.6 0.0 copy-start.3
  0.6 0.0 copy-start.4
  0.7 0.0 copy-start.5
  0.7 0.0 copy-start.6
  0.7 1.4 %pack.1 = (bf16[128,512]{1,0:T(8,128)(2,1)S(1)}, bf16[128,512]{1,0:T(8,128)(2,1)S(1)}, bf16[128,3072]{1,0:T(8,128)(2,1)S(1)}) custom-call(s32[1]{0:T(128)} %bitcast.me_ref, bf16[128,256]{1,0:T(8,128)(2,1)} %rest_0_.1, bf16[128,256]{1,0:T(8,128)(2,1)} %rest_1_.1, bf16[128,256]{1,0:T(8,128)(2,1)} %rest_2_.1, bf16[128,256]{1,0:T(8,128)(2,1)} %rest_3_.1, ...), custom_call_target="tpu_custom_call" | custom-call | flops 65536 | bytes 2097152 | tf_op jit(solution)/shard_map/pack/pallas_call | solution.py:409
  2.1 3.1 %collective-permute-start.4 = (bf16[128,512]{1,0:T(8,128)(2,1)S(1)}, bf16[128,512]{1,0:T(8,128)(2,1)S(1)}, u32[]{:S(2)}, u32[]{:S(2)}) collective-permute-start(bf16[128,512]{1,0:T(8,128)(2,1)S(1)} %get-tuple-element.22), channel_id=1, source_target_pairs={{0,4},{1,5},{2,6},{3,7},{4,0},{5,1},{6,2},{7,3},{8,12},{9,13},{10,... | collective-permute-start | bytes 393224 | tf_op jit(solution)/shard_map/ppermute | solution.py:451
  5.2 1.5 %collective-permute-start.2 = (bf16[128,512]{1,0:T(8,128)(2,1)S(1)}, bf16[128,512]{1,0:T(8,128)(2,1)S(1)}, u32[]{:S(2)}, u32[]{:S(2)}) collective-permute-start(bf16[128,512]{1,0:T(8,128)(2,1)S(1)} %get-tuple-element.22), channel_id=1, source_target_pairs={{0,2},{1,3},{2,0},{3,1},{4,6},{5,7},{6,4},{7,5},{8,10},{9,11},{10,... | collective-permute-start | bytes 393224 | tf_op jit(solution)/shard_map/ppermute | solution.py:451
  6.7 0.0 collective-permute-start.5
  6.7 0.3 collective-permute-start.3
  7.0 0.3 collective-permute-start
  7.3 1.4 %collective-permute-done.4 = bf16[128,512]{1,0:T(8,128)(2,1)S(1)} collective-permute-done((bf16[128,512]{1,0:T(8,128)(2,1)S(1)}, bf16[128,512]{1,0:T(8,128)(2,1)S(1)}, u32[]{:S(2)}, u32[]{:S(2)}) %collective-permute-start.4) | collective-permute-done | bytes 131104 | tf_op jit(solution)/shard_map/ppermute | solution.py:451
  8.7 0.0 copy-start.2
  8.7 3.2 %collective-permute-done.5 = bf16[128,512]{1,0:T(8,128)(2,1)S(1)} collective-permute-done((bf16[128,512]{1,0:T(8,128)(2,1)S(1)}, bf16[128,512]{1,0:T(8,128)(2,1)S(1)}, u32[]{:S(2)}, u32[]{:S(2)}) %collective-permute-start.5) | collective-permute-done | bytes 131104 | tf_op jit(solution)/shard_map/ppermute | solution.py:451
  11.9 0.0 copy-start
  11.9 0.0 copy-start.1
  12.0 1.1 %collective-permute-start.6 = (bf16[2,128,256]{2,1,0:T(8,128)(2,1)S(1)}, bf16[2,128,256]{2,1,0:T(8,128)(2,1)S(1)}, u32[]{:S(2)}, u32[]{:S(2)}) collective-permute-start(bf16[2,128,256]{2,1,0:T(8,128)(2,1)S(1)} %pad_maximum_fusion.1), channel_id=1, source_target_pairs={{0,2},{1,3},{2,0},{3,1},{4,6},{5,7},{6,4},{7,5},{8,10},{9,11},{10,... | collective-permute-start | bytes 393224 | tf_op jit(solution)/shard_map/ppermute | solution.py:451
  13.1 0.0 collective-permute-done.2
  13.1 0.0 collective-permute-done.3
  13.2 0.6 %collective-permute-start.7 = (bf16[2,128,256]{2,1,0:T(8,128)(2,1)S(1)}, bf16[2,128,256]{2,1,0:T(8,128)(2,1)S(1)}, u32[]{:S(2)}, u32[]{:S(2)}) collective-permute-start(bf16[2,128,256]{2,1,0:T(8,128)(2,1)S(1)} %pad_maximum_fusion.2), channel_id=1, source_target_pairs={{0,4},{1,5},{2,6},{3,7},{4,0},{5,1},{6,2},{7,3},{8,12},{9,13},{10,... | collective-permute-start | bytes 393224 | tf_op jit(solution)/shard_map/ppermute | solution.py:451
  13.8 0.5 collective-permute-start.1
  14.3 2.7 %collective-permute-done.6 = bf16[2,128,256]{2,1,0:T(8,128)(2,1)S(1)} collective-permute-done((bf16[2,128,256]{2,1,0:T(8,128)(2,1)S(1)}, bf16[2,128,256]{2,1,0:T(8,128)(2,1)S(1)}, u32[]{:S(2)}, u32[]{:S(2)}) %collective-permute-start.6) | collective-permute-done | bytes 131104 | tf_op jit(solution)/shard_map/ppermute | solution.py:451
  17.0 1.5 %collective-permute-done.7 = bf16[2,128,256]{2,1,0:T(8,128)(2,1)S(1)} collective-permute-done((bf16[2,128,256]{2,1,0:T(8,128)(2,1)S(1)}, bf16[2,128,256]{2,1,0:T(8,128)(2,1)S(1)}, u32[]{:S(2)}, u32[]{:S(2)}) %collective-permute-start.7) | collective-permute-done | bytes 131104 | tf_op jit(solution)/shard_map/ppermute | solution.py:451
  18.5 0.0 collective-permute-done.1
  18.5 0.0 collective-permute-done.peer_ref
  18.5 0.0 copy-done.3
  18.6 0.0 copy-done.4
  18.6 0.0 copy-done.5
  18.6 0.0 copy-done.6
  18.6 0.0 copy-done.2
  18.6 0.0 copy-done
  18.6 0.0 copy-done.1
  18.6 9.7 %hvp.1 = (bf16[2,128,1024]{2,1,0:T(8,128)(2,1)S(1)}, f32[8,128]{1,0:T(8,128)S(1)}, f32[256,256]{1,0:T(8,128)S(1)}, bf16[256,256]{1,0:T(8,128)(2,1)S(1)}, bf16[25...) custom-call(s32[1]{0:T(128)} %bitcast.me_ref, s32[8]{0:T(128)} %order_hbm.1, bf16[128,2048]{1,0:T(8,128)(2,1)S(1)} %copy-done, ...), custom_call_target="tpu_custom_call" | custom-call | flops 2684354560 | bytes 4194304 | tf_op jit(solution)/shard_map/hvp/pallas_call | solution.py:294
  28.4 0.1 collective-permute-start.11
  28.5 3.1 %collective-permute-start.8 = (bf16[256,256]{1,0:T(8,128)(2,1)S(1)}, bf16[256,256]{1,0:T(8,128)(2,1)S(1)}, u32[]{:S(2)}, u32[]{:S(2)}) collective-permute-start(bf16[256,256]{1,0:T(8,128)(2,1)S(1)} %get-tuple-element.24), channel_id=1, source_target_pairs={{0,2},{1,3},{2,0},{3,1},{4,6},{5,7},{6,4},{7,5},{8,10},{9,11},{10,... | collective-permute-start | bytes 393224 | tf_op jit(solution)/shard_map/ppermute | solution.py:451
  31.5 1.9 %collective-permute-start.9 = (bf16[256,256]{1,0:T(8,128)(2,1)S(1)}, bf16[256,256]{1,0:T(8,128)(2,1)S(1)}, u32[]{:S(2)}, u32[]{:S(2)}) collective-permute-start(bf16[256,256]{1,0:T(8,128)(2,1)S(1)} %get-tuple-element.25), channel_id=1, source_target_pairs={{0,4},{1,5},{2,6},{3,7},{4,0},{5,1},{6,2},{7,3},{8,12},{9,13},{10,... | collective-permute-start | bytes 393224 | tf_op jit(solution)/shard_map/ppermute | solution.py:451
  33.4 1.4 %collective-permute-start.10 = (bf16[256,256]{1,0:T(8,128)(2,1)S(1)}, bf16[256,256]{1,0:T(8,128)(2,1)S(1)}, u32[]{:S(2)}, u32[]{:S(2)}) collective-permute-start(bf16[256,256]{1,0:T(8,128)(2,1)S(1)} %get-tuple-element.26), channel_id=1, source_target_pairs={{0,6},{1,7},{2,4},{3,5},{4,2},{5,3},{6,0},{7,1},{8,14},{9,15},{10,... | collective-permute-start | bytes 393224 | tf_op jit(solution)/shard_map/ppermute | solution.py:451
  34.8 0.8 %collective-permute-done.8.rest_0_ = bf16[256,256]{1,0:T(8,128)(2,1)S(1)} collective-permute-done((bf16[256,256]{1,0:T(8,128)(2,1)S(1)}, bf16[256,256]{1,0:T(8,128)(2,1)S(1)}, u32[]{:S(2)}, u32[]{:S(2)}) %collective-permute-start.8) | collective-permute-done | bytes 131104 | tf_op jit(solution)/shard_map/ppermute | solution.py:451
  35.6 3.9 %collective-permute-done.9.rest_1_ = bf16[256,256]{1,0:T(8,128)(2,1)S(1)} collective-permute-done((bf16[256,256]{1,0:T(8,128)(2,1)S(1)}, bf16[256,256]{1,0:T(8,128)(2,1)S(1)}, u32[]{:S(2)}, u32[]{:S(2)}) %collective-permute-start.9) | collective-permute-done | bytes 131104 | tf_op jit(solution)/shard_map/ppermute | solution.py:451
  39.5 1.9 %collective-permute-done.10.rest_2_ = bf16[256,256]{1,0:T(8,128)(2,1)S(1)} collective-permute-done((bf16[256,256]{1,0:T(8,128)(2,1)S(1)}, bf16[256,256]{1,0:T(8,128)(2,1)S(1)}, u32[]{:S(2)}, u32[]{:S(2)}) %collective-permute-start.10) | collective-permute-done | bytes 131104 | tf_op jit(solution)/shard_map/ppermute | solution.py:451
  41.4 0.0 collective-permute-done.11.rest_4_
  41.4 0.8 %add.1 = (bf16[128,2048]{1,0:T(8,128)(2,1)}, bf16[128,256]{1,0:T(8,128)(2,1)S(1)}, bf16[128,256]{1,0:T(8,128)(2,1)S(1)}, f32[32,1,128]{2,1,0:T(1,128)S(1)}) custom-call(s32[1]{0:T(128)} %bitcast.me_ref, f32[256,256]{1,0:T(8,128)S(1)} %get-tuple-element.23.own_ref, bf16[256,256]{1,0:T(8,128)(2,1)S(1)} %collective-permute-done.8.rest_0_, ...), custom_call_target="tpu_custom_call" | custom-call | flops 1048576 | bytes 2097152 | tf_op jit(solution)/shard_map/add/pallas_call | solution.py:356
  42.2 0.1 collective-permute-start.12
  42.3 12.2 %all_to_all.5.lines_ref = f32[32,1,128]{2,1,0:T(1,128)S(1)} all-to-all(f32[32,1,128]{2,1,0:T(1,128)S(1)} %get-tuple-element.32), channel_id=1, replica_groups=mesh['head'=4,'seq'=8] {'head','seq'}, dimensions={0} | all-to-all | bytes 32768 | tf_op jit(solution)/shard_map/all_to_all | solution.py:523
  54.5 0.0 collective-permute-done.12.got_ref
  54.5 0.7 %last.1 = (bf16[128,256]{1,0:T(8,128)(2,1)}, bf16[128,256]{1,0:T(8,128)(2,1)}, f32[1,1]{1,0:T(1,128)}) custom-call(s32[1]{0:T(128)} %bitcast.me_ref, bf16[128,256]{1,0:T(8,128)(2,1)S(1)} %get-tuple-element.30.mine_ref, bf16[128,256]{1,0:T(8,128)(2,1)S(1)} %collective-permute-done.12.got_ref, f32[32,1,128]{2,1,0:T(1,128)S(1)} %all_to_all.5.lines_ref), custom_call_target="tpu_custom_call" | custom-call | flops 65536 | bytes 262144 | tf_op jit(solution)/shard_map/last/pallas_call | solution.py:432
  (8 shorter events, 0.1 us)
Async XLA Ops:
  0.6 17.9 %copy-start.3 = (bf16[128,256]{1,0:T(8,128)(2,1)S(1)}, bf16[128,256]{1,0:T(8,128)(2,1)}, u32[]{:S(2)}) copy-start(bf16[128,256]{1,0:T(8,128)(2,1)} %rest_0_.1) | copy-start | bytes 196612
  0.6 17.9 %copy-start.4 = (bf16[128,256]{1,0:T(8,128)(2,1)S(1)}, bf16[128,256]{1,0:T(8,128)(2,1)}, u32[]{:S(2)}) copy-start(bf16[128,256]{1,0:T(8,128)(2,1)} %rest_1_.1) | copy-start | bytes 196612
  0.7 17.9 %copy-start.5 = (bf16[128,256]{1,0:T(8,128)(2,1)S(1)}, bf16[128,256]{1,0:T(8,128)(2,1)}, u32[]{:S(2)}) copy-start(bf16[128,256]{1,0:T(8,128)(2,1)} %rest_2_.1) | copy-start | bytes 196612
  0.7 17.9 %copy-start.6 = (bf16[128,256]{1,0:T(8,128)(2,1)S(1)}, bf16[128,256]{1,0:T(8,128)(2,1)}, u32[]{:S(2)}) copy-start(bf16[128,256]{1,0:T(8,128)(2,1)} %rest_3_.1) | copy-start | bytes 196612
  2.1 6.6 %collective-permute-start.4 = (bf16[128,512]{1,0:T(8,128)(2,1)S(1)}, bf16[128,512]{1,0:T(8,128)(2,1)S(1)}, u32[]{:S(2)}, u32[]{:S(2)}) collective-permute-start(bf16[128,512]{1,0:T(8,128)(2,1)S(1)} %get-tuple-element.22), channel_id=1, source_target_pairs={{0,4},{1,5},{2,6},{3,7},{4,0},{5,1},{6,2},{7,3},{8,12},{9,13},{10,... | collective-permute-start | bytes 393224 | tf_op jit(solution)/shard_map/ppermute | solution.py:451
  5.2 7.9 %collective-permute-start.2 = (bf16[128,512]{1,0:T(8,128)(2,1)S(1)}, bf16[128,512]{1,0:T(8,128)(2,1)S(1)}, u32[]{:S(2)}, u32[]{:S(2)}) collective-permute-start(bf16[128,512]{1,0:T(8,128)(2,1)S(1)} %get-tuple-element.22), channel_id=1, source_target_pairs={{0,2},{1,3},{2,0},{3,1},{4,6},{5,7},{6,4},{7,5},{8,10},{9,11},{10,... | collective-permute-start | bytes 393224 | tf_op jit(solution)/shard_map/ppermute | solution.py:451
  6.7 5.3 %collective-permute-start.5 = (bf16[128,512]{1,0:T(8,128)(2,1)S(1)}, bf16[128,512]{1,0:T(8,128)(2,1)S(1)}, u32[]{:S(2)}, u32[]{:S(2)}) collective-permute-start(bf16[128,512]{1,0:T(8,128)(2,1)S(1)} %get-tuple-element.21), channel_id=1, source_target_pairs={{0,5},{1,4},{2,7},{3,6},{4,1},{5,0},{6,3},{7,2},{8,13},{9,12},{10,... | collective-permute-start | bytes 393224 | tf_op jit(solution)/shard_map/ppermute | solution.py:451
  6.7 6.5 %collective-permute-start.3 = (bf16[128,512]{1,0:T(8,128)(2,1)S(1)}, bf16[128,512]{1,0:T(8,128)(2,1)S(1)}, u32[]{:S(2)}, u32[]{:S(2)}) collective-permute-start(bf16[128,512]{1,0:T(8,128)(2,1)S(1)} %get-tuple-element.21), channel_id=1, source_target_pairs={{0,3},{1,2},{2,1},{3,0},{4,7},{5,6},{6,5},{7,4},{8,11},{9,10},{10,... | collective-permute-start | bytes 393224 | tf_op jit(solution)/shard_map/ppermute | solution.py:451
  7.0 11.5 %collective-permute-start = (bf16[128,3072]{1,0:T(8,128)(2,1)S(1)}, bf16[128,3072]{1,0:T(8,128)(2,1)S(1)}, u32[]{:S(2)}, u32[]{:S(2)}) collective-permute-start(bf16[128,3072]{1,0:T(8,128)(2,1)S(1)} %get-tuple-element.20), channel_id=1, source_target_pairs={{0,1},{1,0},{2,3},{3,2},{4,5},{5,4},{6,7},{7,6},{8,9},{9,8},{10,11... | collective-permute-start | bytes 2359304 | tf_op jit(solution)/shard_map/ppermute | solution.py:451
  8.7 9.9 %copy-start.2 = (bf16[128,2048]{1,0:T(8,128)(2,1)S(1)}, bf16[128,2048]{1,0:T(8,128)(2,1)}, u32[]{:S(2)}) copy-start(bf16[128,2048]{1,0:T(8,128)(2,1)} %do_ref.1) | copy-start | bytes 1572868
  11.9 6.7 %copy-start = (bf16[128,2048]{1,0:T(8,128)(2,1)S(1)}, bf16[128,2048]{1,0:T(8,128)(2,1)}, u32[]{:S(2)}) copy-start(bf16[128,2048]{1,0:T(8,128)(2,1)} %q_ref.1) | copy-start | bytes 1572868
  11.9 6.7 %copy-start.1 = (bf16[128,2048]{1,0:T(8,128)(2,1)S(1)}, bf16[128,2048]{1,0:T(8,128)(2,1)}, u32[]{:S(2)}) copy-start(bf16[128,2048]{1,0:T(8,128)(2,1)} %qt_ref.1) | copy-start | bytes 1572868
  12.0 5.0 %collective-permute-start.6 = (bf16[2,128,256]{2,1,0:T(8,128)(2,1)S(1)}, bf16[2,128,256]{2,1,0:T(8,128)(2,1)S(1)}, u32[]{:S(2)}, u32[]{:S(2)}) collective-permute-start(bf16[2,128,256]{2,1,0:T(8,128)(2,1)S(1)} %pad_maximum_fusion.1), channel_id=1, source_target_pairs={{0,2},{1,3},{2,0},{3,1},{4,6},{5,7},{6,4},{7,5},{8,10},{9,11},{10,... | collective-permute-start | bytes 393224 | tf_op jit(solution)/shard_map/ppermute | solution.py:451
  13.2 5.3 %collective-permute-start.7 = (bf16[2,128,256]{2,1,0:T(8,128)(2,1)S(1)}, bf16[2,128,256]{2,1,0:T(8,128)(2,1)S(1)}, u32[]{:S(2)}, u32[]{:S(2)}) collective-permute-start(bf16[2,128,256]{2,1,0:T(8,128)(2,1)S(1)} %pad_maximum_fusion.2), channel_id=1, source_target_pairs={{0,4},{1,5},{2,6},{3,7},{4,0},{5,1},{6,2},{7,3},{8,12},{9,13},{10,... | collective-permute-start | bytes 393224 | tf_op jit(solution)/shard_map/ppermute | solution.py:451
  13.8 4.7 %collective-permute-start.1 = (bf16[128,512]{1,0:T(8,128)(2,1)S(1)}, bf16[128,512]{1,0:T(8,128)(2,1)S(1)}, u32[]{:S(2)}, u32[]{:S(2)}) collective-permute-start(bf16[128,512]{1,0:T(8,128)(2,1)S(1)} %get-tuple-element.21), channel_id=1, source_target_pairs={{0,1},{1,0},{2,3},{3,2},{4,5},{5,4},{6,7},{7,6},{8,9},{9,8},{10,11... | collective-permute-start | bytes 393224 | tf_op jit(solution)/shard_map/ppermute | solution.py:451
  28.4 13.0 %collective-permute-start.11 = (bf16[128,1024]{1,0:T(8,128)(2,1)S(1)}, bf16[128,1024]{1,0:T(8,128)(2,1)S(1)}, u32[]{:S(2)}, u32[]{:S(2)}) collective-permute-start(bf16[128,1024]{1,0:T(8,128)(2,1)S(1)} %slice_bitcast_fusion), channel_id=1, source_target_pairs={{0,1},{1,0},{2,3},{3,2},{4,5},{5,4},{6,7},{7,6},{8,9},{9,8},{10,11... | collective-permute-start | bytes 786440 | tf_op jit(solution)/shard_map/ppermute | solution.py:451
  28.5 7.2 %collective-permute-start.8 = (bf16[256,256]{1,0:T(8,128)(2,1)S(1)}, bf16[256,256]{1,0:T(8,128)(2,1)S(1)}, u32[]{:S(2)}, u32[]{:S(2)}) collective-permute-start(bf16[256,256]{1,0:T(8,128)(2,1)S(1)} %get-tuple-element.24), channel_id=1, source_target_pairs={{0,2},{1,3},{2,0},{3,1},{4,6},{5,7},{6,4},{7,5},{8,10},{9,11},{10,... | collective-permute-start | bytes 393224 | tf_op jit(solution)/shard_map/ppermute | solution.py:451
  31.5 8.0 %collective-permute-start.9 = (bf16[256,256]{1,0:T(8,128)(2,1)S(1)}, bf16[256,256]{1,0:T(8,128)(2,1)S(1)}, u32[]{:S(2)}, u32[]{:S(2)}) collective-permute-start(bf16[256,256]{1,0:T(8,128)(2,1)S(1)} %get-tuple-element.25), channel_id=1, source_target_pairs={{0,4},{1,5},{2,6},{3,7},{4,0},{5,1},{6,2},{7,3},{8,12},{9,13},{10,... | collective-permute-start | bytes 393224 | tf_op jit(solution)/shard_map/ppermute | solution.py:451
  33.4 8.0 %collective-permute-start.10 = (bf16[256,256]{1,0:T(8,128)(2,1)S(1)}, bf16[256,256]{1,0:T(8,128)(2,1)S(1)}, u32[]{:S(2)}, u32[]{:S(2)}) collective-permute-start(bf16[256,256]{1,0:T(8,128)(2,1)S(1)} %get-tuple-element.26), channel_id=1, source_target_pairs={{0,6},{1,7},{2,4},{3,5},{4,2},{5,3},{6,0},{7,1},{8,14},{9,15},{10,... | collective-permute-start | bytes 393224 | tf_op jit(solution)/shard_map/ppermute | solution.py:451
  42.2 12.3 %collective-permute-start.12 = (bf16[128,256]{1,0:T(8,128)(2,1)S(1)}, bf16[128,256]{1,0:T(8,128)(2,1)S(1)}, u32[]{:S(2)}, u32[]{:S(2)}) collective-permute-start(bf16[128,256]{1,0:T(8,128)(2,1)S(1)} %get-tuple-element.31), channel_id=1, source_target_pairs={{0,1},{1,0},{2,3},{3,2},{4,5},{5,4},{6,7},{7,6},{8,9},{9,8},{10,11... | collective-permute-start | bytes 196616 | tf_op jit(solution)/shard_map/ppermute | solution.py:451
